TPU v7x, 32 devices: a whole 2x2x4 slice. The times are simulated.
32 devices in a mesh: dp: 8 (over z, y), seq: 4 (over x, core).
Axes of the slice: x: 2, y: 2, z: 4, core: 2. Of those that a mesh axis runs over, the one named last changes fastest.
Arguments:
- decoder_in: bfloat16 [8, 512, 1024], P('dp', 'seq'), may hold values from -6 to 6
- encoder_states: bfloat16 [8, 1024, 1024], P('dp', 'seq'), may hold values from -6 to 6
- out_grad: bfloat16 [8, 512, 1024], P('dp', 'seq'), may hold values from -6 to 6
- seq_lengths: int32 [8], P('dp'), may hold values from 128 to 512, as said below
- enc_lengths: int32 [8], P('dp'), may hold values from 256 to 1024, as said below
- self_qkv: bfloat16 [3, 1024, 1024], P(None, 'dp'), may hold values from -0.1875 to 0.1875
- self_out: bfloat16 [1024, 1024], P('dp'), may hold values from -1.5 to 1.5
- cross_qkv: bfloat16 [3, 1024, 1024], P(None, 'dp'), may hold values from -0.1875 to 0.1875
- cross_out: bfloat16 [1024, 1024], P('dp'), may hold values from -1.5 to 1.5
- attn_bias: bfloat16 [6, 1024], P(None, 'dp'), may hold values from -3 to 3
- ffn_in: bfloat16 [1024, 4096], P('dp'), may hold values from -0.1875 to 0.1875
- ffn_in_bias: bfloat16 [4096], P('dp'), may hold values from -3 to 3
- ffn_out: bfloat16 [4096, 1024], P('dp'), may hold values from -0.09375 to 0.09375
- ffn_out_bias: bfloat16 [1024], P('dp'), may hold values from -3 to 3
- norm_gain: bfloat16 [3, 1024], P(None, 'dp'), may hold values from 0.5 to 1.5
- norm_bias: bfloat16 [3, 1024], P(None, 'dp'), may hold values from -2 to 2
Outputs:
- layer_out: bfloat16 [8, 512, 1024], P('dp', 'seq')
- grad_input: bfloat16 [8, 512, 1024], P('dp', 'seq')
- grad_encoder: bfloat16 [8, 1024, 1024], P('dp', 'seq')
- grad_self_qkv: float32 [3, 1024, 1024], P(None, 'dp')
- grad_self_out: float32 [1024, 1024], P('dp')
- grad_cross_qkv: float32 [3, 1024, 1024], P(None, 'dp')
- grad_cross_out: float32 [1024, 1024], P('dp')
- grad_attn_bias: float32 [6, 1024], P(None, 'dp')
- grad_ffn_in: float32 [1024, 4096], P('dp')
- grad_ffn_in_bias: float32 [4096], P('dp')
- grad_ffn_out: float32 [4096, 1024], P('dp')
- grad_ffn_out_bias: float32 [1024], P('dp')
- grad_norm_gain: float32 [3, 1024], P(None, 'dp')
- grad_norm_bias: float32 [3, 1024], P(None, 'dp')
Inputs may be any that keep to these rules, and one draw needn't show every extreme that they name: Sequence s has seq_lengths[s] real positions at its start, the rest is padding; some sequence is full. Sequence s has enc_lengths[s] real encoder positions at its start; some sequence's encoder states are full.
All inputs are finite; a program needn't handle non-finite values.
Results may differ from a plain program's by a relative error of at most 0.033.
Values may be sent and summed in bfloat16 or wider, within the bound.
A program may use at most 320 MiB of HBM per device.

v0:
```python
import jax
import jax.numpy as jnp
from jax import lax
from jax.sharding import PartitionSpec as P

HD = 64


norm_eps = 1e-05


def gelu_exact(pre_values):
    return 0.5 * pre_values * (1.0 + lax.erf(pre_values * 0.7071067811865476))


def layer_norm(inputs, gain_row, shift_row):
    row_mean = jnp.mean(inputs, axis=-1, keepdims=True)
    centred = inputs - row_mean
    variance = jnp.mean(centred * centred, axis=-1, keepdims=True)
    inv_std = lax.rsqrt(variance + norm_eps)
    normed = centred * inv_std
    return (normed * gain_row + shift_row, normed, inv_std)


def norm_backward(grad_out, normed, inv_std, gain_row):
    grad_gain = jnp.sum(grad_out * normed, axis=0)
    grad_shift = jnp.sum(grad_out, axis=0)
    grad_normed = grad_out * gain_row
    grad_in = inv_std * (
        grad_normed
        - jnp.mean(grad_normed, axis=-1, keepdims=True)
        - normed * jnp.mean(grad_normed * normed, axis=-1, keepdims=True)
    )
    return (grad_gain, grad_shift, grad_in)


def key_mask(row_ids, col_ids, causal, key_limit):
    if causal:
        return col_ids[None, :] <= row_ids[:, None]
    return jnp.broadcast_to(col_ids[None, :] < key_limit, (row_ids.shape[0], col_ids.shape[0]))


def pack_grads(grad_list, dim_list, pieces):
    blocks = []
    for grad_arr, shard_dim in zip(grad_list, dim_list):
        moved = jnp.moveaxis(grad_arr, shard_dim, 0)
        blocks.append(moved.reshape(pieces, -1))
    return jnp.concatenate(blocks, axis=1)


def unpack_grads(packed, grad_list, dim_list, pieces, dp_count):
    results = []
    offset = 0
    for grad_arr, shard_dim in zip(grad_list, dim_list):
        moved_shape = jnp.moveaxis(grad_arr, shard_dim, 0).shape
        per_piece = grad_arr.size // pieces
        column_part = packed[:, offset : offset + per_piece]
        offset = offset + per_piece
        shard_rows = moved_shape[0] // dp_count
        rebuilt = column_part.reshape((shard_rows,) + tuple(moved_shape[1:]))
        results.append(jnp.moveaxis(rebuilt, 0, shard_dim))
    return results


def attend_forward(queries, keys_in, values_in, causal, key_limit):
    total_rows = queries.shape[0]
    head_count = queries.shape[1] // HD
    block_rows = min(512, total_rows)
    block_count = total_rows // block_rows
    score_scale = HD ** (-0.5)
    keys3 = keys_in.reshape(keys_in.shape[0], head_count, HD)
    values3 = values_in.reshape(values_in.shape[0], head_count, HD)
    col_ids = jnp.arange(keys_in.shape[0], dtype=jnp.int32)
    q_blocks = queries.reshape(block_count, block_rows, head_count, HD)

    def one_block(block_item):
        start_row, q_block = block_item
        row_ids = start_row + jnp.arange(block_rows, dtype=jnp.int32)
        allowed = key_mask(row_ids, col_ids, causal, key_limit)
        scores = (
            jnp.einsum("qhd,khd->hqk", q_block, keys3, preferred_element_type=jnp.float32)
            * score_scale
        )
        scores = jnp.where(allowed[None], scores, -1e30)
        row_top = jnp.max(scores, axis=-1, keepdims=True)
        expo_terms = jnp.exp(scores - row_top)
        row_total = jnp.sum(expo_terms, axis=-1, keepdims=True)
        probabilities = (expo_terms / row_total).astype(jnp.bfloat16)
        block_out = jnp.einsum(
            "hqk,khd->qhd", probabilities, values3, preferred_element_type=jnp.float32
        )
        return (
            block_out.astype(jnp.bfloat16).reshape(block_rows, head_count * HD),
            (row_top + jnp.log(row_total))[..., 0],
        )

    starts = jnp.arange(block_count, dtype=jnp.int32) * block_rows
    outputs, log_totals = lax.map(one_block, (starts, q_blocks))
    return (outputs.reshape(total_rows, head_count * HD), log_totals)


def attend_backward(queries, keys_in, values_in, grad_out, log_totals, causal, key_limit):
    total_rows = queries.shape[0]
    key_rows = keys_in.shape[0]
    head_count = queries.shape[1] // HD
    block_rows = min(512, total_rows)
    block_count = total_rows // block_rows
    score_scale = HD ** (-0.5)
    keys3 = keys_in.reshape(key_rows, head_count, HD)
    values3 = values_in.reshape(key_rows, head_count, HD)
    col_ids = jnp.arange(key_rows, dtype=jnp.int32)
    q_blocks = queries.reshape(block_count, block_rows, head_count, HD)
    do_blocks = grad_out.reshape(block_count, block_rows, head_count, HD)

    def one_step(carry_in, block_item):
        start_row, q_block, do_block, lse_block = block_item
        row_ids = start_row + jnp.arange(block_rows, dtype=jnp.int32)
        allowed = key_mask(row_ids, col_ids, causal, key_limit)
        scores = (
            jnp.einsum("qhd,khd->hqk", q_block, keys3, preferred_element_type=jnp.float32)
            * score_scale
        )
        scores = jnp.where(allowed[None], scores, -1e30)
        probabilities = jnp.exp(scores - lse_block[..., None])
        probs_low = probabilities.astype(jnp.bfloat16)
        grad_probs = jnp.einsum(
            "qhd,khd->hqk", do_block, values3, preferred_element_type=jnp.float32
        )
        row_delta = jnp.sum(grad_probs * probabilities, axis=-1, keepdims=True)
        grad_scores = (probabilities * (grad_probs - row_delta)).astype(jnp.bfloat16)
        grad_query = (
            jnp.einsum("hqk,khd->qhd", grad_scores, keys3, preferred_element_type=jnp.float32)
            * score_scale
        )
        grad_keys = (
            carry_in[0]
            + jnp.einsum("hqk,qhd->khd", grad_scores, q_block, preferred_element_type=jnp.float32)
            * score_scale
        )
        grad_values = carry_in[1] + jnp.einsum(
            "hqk,qhd->khd", probs_low, do_block, preferred_element_type=jnp.float32
        )
        return ((grad_keys, grad_values), grad_query.reshape(block_rows, head_count * HD))

    starts = jnp.arange(block_count, dtype=jnp.int32) * block_rows
    zero_kv = jnp.zeros((key_rows, head_count, HD), jnp.float32)
    (grad_keys, grad_values), grad_queries = lax.scan(
        one_step, (zero_kv, zero_kv), (starts, q_blocks, do_blocks, log_totals)
    )
    return (
        grad_queries.reshape(total_rows, head_count * HD),
        grad_keys.reshape(key_rows, head_count * HD),
        grad_values.reshape(key_rows, head_count * HD),
    )


def on_device(
    decoder_in,
    encoder_states,
    out_grad,
    seq_lengths,
    enc_lengths,
    self_qkv,
    self_out,
    cross_qkv,
    cross_out,
    attn_bias,
    ffn_in,
    ffn_in_bias,
    ffn_out,
    ffn_out_bias,
    norm_gain,
    norm_bias,
):
    (
        w_sqkv,
        w_sout,
        w_cqkv,
        w_cout,
        biases,
        w_first,
        b_first,
        w_second,
        b_second,
        gain_rows,
        shifts,
    ) = (
        lax.all_gather(self_qkv, "dp", axis=1, tiled=True),
        lax.all_gather(self_out, "dp", axis=0, tiled=True),
        lax.all_gather(cross_qkv, "dp", axis=1, tiled=True),
        lax.all_gather(cross_out, "dp", axis=0, tiled=True),
        lax.all_gather(attn_bias, "dp", axis=1, tiled=True),
        lax.all_gather(ffn_in, "dp", axis=0, tiled=True),
        lax.all_gather(ffn_in_bias, "dp", axis=0, tiled=True),
        lax.all_gather(ffn_out, "dp", axis=0, tiled=True),
        lax.all_gather(ffn_out_bias, "dp", axis=0, tiled=True),
        lax.all_gather(norm_gain, "dp", axis=1, tiled=True),
        lax.all_gather(norm_bias, "dp", axis=1, tiled=True),
    )
    bias32 = biases.astype(jnp.float32)
    gain32 = gain_rows.astype(jnp.float32)
    shift32 = shifts.astype(jnp.float32)
    tokens = decoder_in[0]
    states = encoder_states[0]
    seq_len = seq_lengths[0]
    enc_len = enc_lengths[0]
    tok_rows = tokens.shape[0]
    width = tokens.shape[1]
    zero_row = jnp.zeros((width,), jnp.float32)
    projected = jnp.einsum("td,cde->cte", tokens, w_sqkv, preferred_element_type=jnp.float32)
    self_bias_rows = jnp.stack([bias32[0], zero_row, bias32[1]])[:, None, :]
    qkv_low = (projected + self_bias_rows).astype(jnp.bfloat16)
    head_qkv = lax.all_to_all(qkv_low, "seq", split_axis=2, concat_axis=1, tiled=True)
    self_heads_out, self_lse = attend_forward(head_qkv[0], head_qkv[1], head_qkv[2], True, seq_len)
    mixed_out = lax.all_to_all(self_heads_out, "seq", split_axis=0, concat_axis=1, tiled=True)
    row_ids = lax.axis_index("seq") * tok_rows + jnp.arange(tok_rows, dtype=jnp.int32)
    row_scale = (row_ids < seq_len).astype(jnp.float32)[:, None]
    branch = jnp.dot(mixed_out, w_sout, preferred_element_type=jnp.float32) + bias32[2]
    first_out, normed_one, inv_one = layer_norm(
        tokens.astype(jnp.float32) + branch, gain32[0], shift32[0]
    )
    first_low = first_out.astype(jnp.bfloat16)
    cross_query = (
        jnp.dot(first_low, w_cqkv[0], preferred_element_type=jnp.float32) + bias32[3]
    ).astype(jnp.bfloat16)
    cross_bias_rows = jnp.stack([zero_row, bias32[4]])[:, None, :]
    cross_kv = (
        jnp.einsum("td,cde->cte", states, w_cqkv[1:], preferred_element_type=jnp.float32)
        + cross_bias_rows
    ).astype(jnp.bfloat16)
    head_cq, head_ckv = (
        lax.all_to_all(cross_query[None], "seq", split_axis=2, concat_axis=1, tiled=True),
        lax.all_to_all(cross_kv, "seq", split_axis=2, concat_axis=1, tiled=True),
    )
    cross_heads_out, cross_lse = attend_forward(
        head_cq[0], head_ckv[0], head_ckv[1], False, enc_len
    )
    mixed_two = lax.all_to_all(cross_heads_out, "seq", split_axis=0, concat_axis=1, tiled=True)
    branch_two = jnp.dot(mixed_two, w_cout, preferred_element_type=jnp.float32) + bias32[5]
    second, normed_two, inv_two = layer_norm(first_out + branch_two, gain32[1], shift32[1])
    second_low = second.astype(jnp.bfloat16)
    pre_act = jnp.dot(second_low, w_first, preferred_element_type=jnp.float32) + b_first.astype(
        jnp.float32
    )
    act_value, act_pullback = jax.vjp(gelu_exact, pre_act)
    hidden = act_value.astype(jnp.bfloat16)
    branch_three = jnp.dot(hidden, w_second, preferred_element_type=jnp.float32) + b_second.astype(
        jnp.float32
    )
    third_out, normed_three, inv_three = layer_norm(second + branch_three, gain32[2], shift32[2])
    layer_out = (third_out * row_scale).astype(jnp.bfloat16)[None]
    grad_third = out_grad[0].astype(jnp.float32) * row_scale
    grad_gain3, grad_shift3, grad_h3 = norm_backward(grad_third, normed_three, inv_three, gain32[2])
    grad_y3 = grad_h3.astype(jnp.bfloat16)
    grad_w_second = jnp.einsum("tf,td->fd", hidden, grad_y3, preferred_element_type=jnp.float32)
    grad_b_second = jnp.sum(grad_y3.astype(jnp.float32), axis=0)
    grad_hidden = jnp.einsum("td,fd->tf", grad_y3, w_second, preferred_element_type=jnp.float32)
    grad_pre = act_pullback(grad_hidden)[0].astype(jnp.bfloat16)
    grad_w_first = jnp.einsum("td,tf->df", second_low, grad_pre, preferred_element_type=jnp.float32)
    grad_b_first = jnp.sum(grad_pre.astype(jnp.float32), axis=0)
    grad_second = grad_h3 + jnp.einsum(
        "tf,df->td", grad_pre, w_first, preferred_element_type=jnp.float32
    )
    grad_gain2, grad_shift2, grad_h2 = norm_backward(grad_second, normed_two, inv_two, gain32[1])
    grad_y2 = grad_h2.astype(jnp.bfloat16)
    grad_w_cout = jnp.einsum("td,te->de", mixed_two, grad_y2, preferred_element_type=jnp.float32)
    grad_bias_cout = jnp.sum(grad_y2.astype(jnp.float32), axis=0)
    grad_mixed_two = jnp.einsum(
        "te,de->td", grad_y2, w_cout, preferred_element_type=jnp.float32
    ).astype(jnp.bfloat16)
    grad_cross_heads = lax.all_to_all(
        grad_mixed_two, "seq", split_axis=1, concat_axis=0, tiled=True
    )
    cq_grad, ck_grad, cv_grad = attend_backward(
        head_cq[0], head_ckv[0], head_ckv[1], grad_cross_heads, cross_lse, False, enc_len
    )
    back_q, back_kv = (
        lax.all_to_all(
            cq_grad.astype(jnp.bfloat16)[None], "seq", split_axis=1, concat_axis=2, tiled=True
        ),
        lax.all_to_all(
            jnp.stack([ck_grad, cv_grad]).astype(jnp.bfloat16),
            "seq",
            split_axis=1,
            concat_axis=2,
            tiled=True,
        ),
    )
    grad_w_cq = jnp.einsum("td,te->de", first_low, back_q[0], preferred_element_type=jnp.float32)
    grad_w_ckv = jnp.einsum("td,cte->cde", states, back_kv, preferred_element_type=jnp.float32)
    grad_w_cqkv = jnp.concatenate([grad_w_cq[None], grad_w_ckv], axis=0)
    grad_cbias_q = jnp.sum(back_q[0].astype(jnp.float32), axis=0)
    grad_cbias_v = jnp.sum(back_kv[1].astype(jnp.float32), axis=0)
    grad_encoder = jnp.einsum(
        "cte,cde->td", back_kv, w_cqkv[1:], preferred_element_type=jnp.float32
    ).astype(jnp.bfloat16)[None]
    grad_first = grad_h2 + jnp.einsum(
        "te,de->td", back_q[0], w_cqkv[0], preferred_element_type=jnp.float32
    )
    grad_gain1, grad_shift1, grad_h1 = norm_backward(grad_first, normed_one, inv_one, gain32[0])
    grad_y1 = grad_h1.astype(jnp.bfloat16)
    grad_w_sout = jnp.einsum("td,te->de", mixed_out, grad_y1, preferred_element_type=jnp.float32)
    grad_bias_sout = jnp.sum(grad_y1.astype(jnp.float32), axis=0)
    grad_mixed = jnp.einsum(
        "te,de->td", grad_y1, w_sout, preferred_element_type=jnp.float32
    ).astype(jnp.bfloat16)
    grad_self_heads = lax.all_to_all(grad_mixed, "seq", split_axis=1, concat_axis=0, tiled=True)
    sq_grad, sk_grad, sv_grad = attend_backward(
        head_qkv[0], head_qkv[1], head_qkv[2], grad_self_heads, self_lse, True, seq_len
    )
    back_self = lax.all_to_all(
        jnp.stack([sq_grad, sk_grad, sv_grad]).astype(jnp.bfloat16),
        "seq",
        split_axis=1,
        concat_axis=2,
        tiled=True,
    )
    grad_w_sqkv = jnp.einsum("td,cte->cde", tokens, back_self, preferred_element_type=jnp.float32)
    grad_sbias_q = jnp.sum(back_self[0].astype(jnp.float32), axis=0)
    grad_sbias_v = jnp.sum(back_self[2].astype(jnp.float32), axis=0)
    grad_input = (
        grad_h1 + jnp.einsum("cte,cde->td", back_self, w_sqkv, preferred_element_type=jnp.float32)
    ).astype(jnp.bfloat16)[None]
    grad_biases = jnp.stack(
        [grad_sbias_q, grad_sbias_v, grad_bias_sout, grad_cbias_q, grad_cbias_v, grad_bias_cout]
    )
    grad_gains = jnp.stack([grad_gain1, grad_gain2, grad_gain3])
    grad_shifts = jnp.stack([grad_shift1, grad_shift2, grad_shift3])
    weight_dims = (1, 0, 1, 0, 1, 0, 0, 0, 0, 1, 1)
    grad_list = [
        grad_w_sqkv,
        grad_w_sout,
        grad_w_cqkv,
        grad_w_cout,
        grad_biases,
        grad_w_first,
        grad_b_first,
        grad_w_second,
        grad_b_second,
        grad_gains,
        grad_shifts,
    ]
    dp_count = lax.axis_size("dp")
    seq_count = lax.axis_size("seq")
    piece_count = dp_count * seq_count
    packed = pack_grads(grad_list, weight_dims, piece_count)
    grouped = packed.reshape(dp_count, -1)
    share = lax.psum_scatter(grouped.astype(jnp.bfloat16), "dp", scatter_dimension=0, tiled=True)
    summed = lax.psum(share, "seq").astype(jnp.float32).reshape(seq_count, -1)
    outs = unpack_grads(summed, grad_list, weight_dims, piece_count, dp_count)
    return (
        layer_out,
        grad_input,
        grad_encoder,
        outs[0],
        outs[1],
        outs[2],
        outs[3],
        outs[4],
        outs[5],
        outs[6],
        outs[7],
        outs[8],
        outs[9],
        outs[10],
    )


def solution(mesh):
    placed = (
        P("dp", "seq", None),
        P("dp", "seq", None),
        P("dp", "seq", None),
        P("dp"),
        P("dp"),
        P(None, "dp", None),
        P("dp", None),
        P(None, "dp", None),
        P("dp", None),
        P(None, "dp"),
        P("dp", None),
        P("dp"),
        P("dp", None),
        P("dp"),
        P(None, "dp"),
        P(None, "dp"),
    )
    return jax.shard_map(
        on_device,
        mesh=mesh,
        in_specs=placed,
        out_specs=(
            P("dp", "seq", None),
            P("dp", "seq", None),
            P("dp", "seq", None),
            P(None, "dp", None),
            P("dp", None),
            P(None, "dp", None),
            P("dp", None),
            P(None, "dp"),
            P("dp", None),
            P("dp"),
            P("dp", None),
            P("dp"),
            P(None, "dp"),
            P(None, "dp"),
        ),
        check_vma=False,
    )
```

profile of v0, /device:TPU:1, one launch (start us, length us, event | category | flops | bytes accessed | tf_op | source)
XLA Modules:
  0.0 2204.0 jit_solution(14434187904151776479)
XLA Ops:
  14.6 18.4 all-gather.1
  33.0 22.7 %all-gather = bf16[8,1,512]{2,1,0:T(2,128)(2,1)S(1)} all-gather(bf16[1,1,512]{2,1,0:T(2,128)(2,1)S(1)} %reshape.344), channel_id=1, replica_groups=mesh['dp'=8,'seq'=4] {'dp'}, dimensions={0}, use_global_device_ids=true | all-gather | bytes 9216 | tf_op jit(solution)/shard_map/all_gather | solution.py:194
  57.0 26.0 %all_gather.34 = bf16[6,1024]{1,0:T(8,128)(2,1)S(1)} all-gather(bf16[6,128]{1,0:T(8,128)(2,1)S(1)} %copy-done.33), channel_id=1, replica_groups=mesh['dp'=8,'seq'=4] {'dp'}, dimensions={1}, use_global_device_ids=true | all-gather | bytes 13824 | tf_op jit(solution)/shard_map/all_gather | solution.py:192
  83.1 17.0 all_gather.37
  100.1 13.4 all_gather.36
  113.7 4.6 fusion.21
  120.0 23.6 %all-to-all-start = ((bf16[3,128,1024]{1,0,2:T(4,128)(2,1)}), bf16[3,128,1024]{1,0,2:T(4,128)(2,1)S(1)}, u32[]{:S(2)}, u32[]{:S(2)}) async-start(bf16[3,128,1024]{1,0,2:T(4,128)(2,1)} %copy.162), calls=%async_computation | async-start | bytes 2097152 | tf_op jit(solution)/shard_map/all_to_all | solution.py:213
  143.6 68.9 %all-gather.13.cloned.1.call-done = bf16[3,1024,1024]{1,2,0:T(8,128)(2,1)} async-done(((bf16[3,128,1024]{1,2,0:T(8,128)(2,1)}), bf16[3,1024,1024]{1,2,0:T(8,128)(2,1)}) %all-gather.13.cloned.1.call-update) | async-done | bytes 6291472 | tf_op jit(solution)/shard_map/all_gather | solution.py:190
  218.0 4.9 all-to-all-start.2
  231.8 4.5 all-to-all-done.2
  236.4 4.6 all-to-all-start.1
  242.8 18.0 all-gather.11.cloned.1.call-done
  269.6 6.0 all-to-all-start.3
  289.3 4.6 all-to-all-start.4
  293.9 16.5 all-gather.15.cloned.1.call-done
  312.9 123.7 %all-gather.17.cloned.1.call-done = bf16[1024,4096]{1,0:T(8,128)(2,1)} async-done(((bf16[128,4096]{1,0:T(8,128)(2,1)}), bf16[1024,4096]{1,0:T(8,128)(2,1)}) %all-gather.17.cloned.1.call-update) | async-done | bytes 8388624 | tf_op jit(solution)/shard_map/all_gather | solution.py:193
  436.7 4.7 convolution_add_fusion
  441.4 119.9 %all-gather.19.cloned.1.call-done = bf16[4096,1024]{1,0:T(8,128)(2,1)} async-done(((bf16[512,1024]{1,0:T(8,128)(2,1)}), bf16[4096,1024]{1,0:T(8,128)(2,1)}) %all-gather.19.cloned.1.call-update) | async-done | bytes 8388624 | tf_op jit(solution)/shard_map/all_gather | solution.py:195
  561.4 4.9 fusion.99
  567.9 5.3 convolution_convert_fusion
  576.8 5.7 convolution_convert_fusion.1
  587.4 4.9 all-to-all-start.5
  596.6 8.9 reshape.324
  605.4 8.9 reshape.326
  614.8 5.0 multiply_reduce_fusion
  619.8 5.2 fusion.22
  625.1 4.7 multiply_convert_fusion
  636.5 4.5 all-to-all-start.6
  673.0 4.3 all-to-all-start.9
  695.5 4.3 all-to-all-start.8
  707.6 14.4 copy.194
  722.0 11.2 reshape.321
  736.2 4.5 convert_bitcast_fusion
  740.8 14.4 copy.191
  755.1 11.2 reshape.319
  766.3 5.9 constant_dynamic-update-slice_fusion.3
  775.8 5.9 constant_dynamic-update-slice_fusion.1
  784.6 46.1 %dynamic-update-slice.5 = bf16[32,524832]{1,0:T(8,128)(2,1)} dynamic-update-slice(bf16[32,524832]{1,0:T(8,128)(2,1)} %dynamic-update-slice.4, bf16[32,131072]{1,0:T(8,128)(2,1)} %reshape.324, s32[]{} %constant.133, s32[]{} %constant.138) | dynamic-update-slice | bytes 16777220
  832.1 45.7 %dynamic-update-slice.7 = bf16[32,524832]{1,0:T(8,128)(2,1)} dynamic-update-slice(bf16[32,524832]{1,0:T(8,128)(2,1)} %dynamic-update-slice.6, bf16[32,131072]{1,0:T(8,128)(2,1)} %reshape.326, s32[]{} %constant.133, s32[]{} %constant.140) | dynamic-update-slice | bytes 16777220
  882.7 66.5 %reshape.357 = bf16[16794624]{0:T(1024)(128)(2,1)} reshape(bf16[32,524832]{1,0:T(8,128)(2,1)} %dynamic-update-slice.10) | data formatting | bytes 67178496
  949.2 59.6 %convert_element_type.218 = bf16[8,2099328]{1,0:T(8,128)(2,1)} reshape(bf16[16794624]{0:T(1024)(128)(2,1)} %reshape.357) | data formatting | bytes 67178496 | tf_op jit(solution)/shard_map/convert_element_type | solution.py:348
  1010.0 971.3 %all-reduce.7.cloned.1.call-done = bf16[8,2099328]{1,0:T(8,128)(2,1)} async-done(((bf16[8,2099328]{1,0:T(8,128)(2,1)}), bf16[8,2099328]{1,0:T(8,128)(2,1)}) %all-reduce.7.cloned.1.call-update) | async-done | bytes 33589264
  1981.4 83.3 %dynamic-slice_reduce_fusion = bf16[2099328]{0:T(1024)(128)(2,1)} fusion(bf16[8,2099328]{1,0:T(8,128)(2,1)} %all-reduce.7.cloned.1.call-done, u32[]{:T(128)} %bitcast.82), kind=kLoop, calls=%fused_computation | loop fusion | bytes 8397316
  2064.7 9.5 reshape.330
  2074.3 4.3 fusion.29
  2078.6 5.2 fusion.50
  2083.8 75.5 %all-reduce.5.cloned.1.call-done = bf16[4,524832]{1,0:T(4,128)(2,1)} async-done(((bf16[4,524832]{1,0:T(4,128)(2,1)}), bf16[4,524832]{1,0:T(4,128)(2,1)}) %all-reduce.5.cloned.1.call-update) | async-done | bytes 4198672 | tf_op jit(solution)/shard_map/psum | solution.py:349
  2181.4 4.4 reshape.337
  (280 shorter events, 179.7 us)
Async XLA Ops:
  7.2 205.3 %copy-start = (bf16[1,256,1024]{2,1,0:T(8,128)(2,1)S(1)}, bf16[1,256,1024]{2,1,0:T(8,128)(2,1)}, u32[]{:S(2)}) copy-start(bf16[1,256,1024]{2,1,0:T(8,128)(2,1)} %param.17) | copy-start | bytes 1572868
  7.2 7.4 copy-start.37
  7.2 25.7 %copy-start.34 = (bf16[512]{0:T(512)(128)(2,1)S(1)}, bf16[512]{0:T(512)(128)(2,1)}, u32[]{:S(2)}) copy-start(bf16[512]{0:T(512)(128)(2,1)} %param.27) | copy-start | bytes 3076
  7.2 49.7 %copy-start.33 = (bf16[6,128]{1,0:T(8,128)(2,1)S(1)}, bf16[6,128]{1,0:T(8,128)(2,1)}, u32[]{:S(2)}) copy-start(bf16[6,128]{1,0:T(8,128)(2,1)} %param.25) | copy-start | bytes 4612
  7.2 75.8 %copy-start.35 = (bf16[3,128]{1,0:T(4,128)(2,1)S(1)}, bf16[3,128]{1,0:T(4,128)(2,1)}, u32[]{:S(2)}) copy-start(bf16[3,128]{1,0:T(4,128)(2,1)} %param.31) | copy-start | bytes 2308
  7.2 92.9 %copy-start.36 = (bf16[3,128]{1,0:T(4,128)(2,1)S(1)}, bf16[3,128]{1,0:T(4,128)(2,1)}, u32[]{:S(2)}) copy-start(bf16[3,128]{1,0:T(4,128)(2,1)} %param.30) | copy-start | bytes 2308
  7.2 106.5 %copy-start.31 = (bf16[1,128,1024]{2,1,0:T(8,128)(2,1)S(1)}, bf16[1,128,1024]{2,1,0:T(8,128)(2,1)}, u32[]{:S(2)}) copy-start(bf16[1,128,1024]{2,1,0:T(8,128)(2,1)} %param.16) | copy-start | bytes 786436
  7.3 106.5 %all-gather.9.cloned.1.call-start = ((), (), s32[]{:S(2)}) async-start(), calls=%async_computation.10 | async-start | bytes 7077888 | tf_op jit(solution)/shard_map/all_gather | solution.py:188
  9.7 202.7 %all-gather.13.cloned.1.call-start = ((), (), s32[]{:S(2)}) async-start(), calls=%async_computation.12 | async-start | bytes 7077888 | tf_op jit(solution)/shard_map/all_gather | solution.py:190
  12.1 248.7 %all-gather.11.cloned.1.call-start = ((), (), s32[]{:S(2)}) async-start(), calls=%async_computation.11 | async-start | bytes 2359296 | tf_op jit(solution)/shard_map/all_gather | solution.py:189
  12.8 297.6 %all-gather.15.cloned.1.call-start = ((), (), s32[]{:S(2)}) async-start(), calls=%async_computation.13 | async-start | bytes 2359296 | tf_op jit(solution)/shard_map/all_gather | solution.py:191
  13.4 423.3 %all-gather.17.cloned.1.call-start = ((), (), s32[]{:S(2)}) async-start(), calls=%async_computation.14 | async-start | bytes 9437184 | tf_op jit(solution)/shard_map/all_gather | solution.py:193
  14.0 547.4 %all-gather.19.cloned.1.call-start = ((), (), s32[]{:S(2)}) async-start(), calls=%async_computation.15 | async-start | bytes 9437184 | tf_op jit(solution)/shard_map/all_gather | solution.py:195
  120.0 98.0 %all-to-all-start = ((bf16[3,128,1024]{1,0,2:T(4,128)(2,1)}), bf16[3,128,1024]{1,0,2:T(4,128)(2,1)S(1)}, u32[]{:S(2)}, u32[]{:S(2)}) async-start(bf16[3,128,1024]{1,0,2:T(4,128)(2,1)} %copy.162), calls=%async_computation | async-start | bytes 2097152 | tf_op jit(solution)/shard_map/all_to_all | solution.py:213
  218.0 18.4 all-to-all-start.2
  224.1 3.7 copy-start.20
  236.4 24.3 %all-to-all-start.1 = ((bf16[4,128,256]{1,2,0:T(8,128)(2,1)}), bf16[4,128,256]{1,2,0:T(8,128)(2,1)S(1)}, u32[]{:S(2)}, u32[]{:S(2)}) async-start(bf16[4,128,256]{1,2,0:T(8,128)(2,1)} %copy.165), calls=%async_computation.1 | async-start | bytes 524288 | tf_op jit(solution)/shard_map/all_to_all | solution.py:215
  260.7 8.1 copy-start.22
  260.7 14.8 copy-start.17
  263.0 47.5 %copy-start.6 = (f32[128,1024]{1,0:T(8,128)}, f32[128,1024]{1,0:T(8,128)S(1)}, u32[]{:S(2)}) copy-start(f32[128,1024]{1,0:T(8,128)S(1)} %get-tuple-element.227) | copy-start | bytes 1572868
  269.6 11.1 all-to-all-start.3
  276.3 8.5 copy-start.25
  276.7 6.1 copy-start.15
  289.3 21.2 all-to-all-start.4
  310.5 126.2 %copy-start.24 = (bf16[4,128,256]{1,2,0:T(8,128)(2,1)}, bf16[4,128,256]{1,2,0:T(8,128)(2,1)S(1)}, u32[]{:S(2)}) copy-start(bf16[4,128,256]{1,2,0:T(8,128)(2,1)S(1)} %all-to-all-done.4) | copy-start | bytes 786436
  561.3 5.1 copy-start.30
  566.5 6.6 slice-start.2
  567.8 5.3 slice-start.3
  567.8 14.7 slice-start
  573.1 9.4 slice-start.1
  587.4 27.1 %all-to-all-start.5 = ((bf16[128,4,256]{2,0,1:T(8,128)(2,1)}), bf16[128,4,256]{2,0,1:T(8,128)(2,1)S(1)}, u32[]{:S(2)}, u32[]{:S(2)}) async-start(bf16[128,4,256]{2,0,1:T(8,128)(2,1)} %bitcast.237), calls=%async_computation.5 | async-start | bytes 524288 | tf_op jit(solution)/shard_map/all_to_all | solution.py:271
  605.4 9.4 copy-start.26
  625.1 6.7 copy-start.16
  636.5 14.8 all-to-all-start.6
  644.9 8.6 copy-start.7
  653.4 4.7 copy-start.23
  655.2 4.8 copy-start.8
  661.7 11.4 all-to-all-start.7
  669.3 8.3 copy-start.29
  673.0 22.5 %all-to-all-start.9 = ((bf16[2,1024,256]{2,0,1:T(2,128)(2,1)}), bf16[2,1024,256]{2,0,1:T(2,128)(2,1)}, u32[]{:S(2)}, u32[]{:S(2)}) async-start(bf16[2,1024,256]{2,0,1:T(2,128)(2,1)} %pad_maximum_fusion.1), calls=%async_computation.9 | async-start | bytes 2097152 | tf_op jit(solution)/shard_map/all_to_all | solution.py:281
  682.3 6.9 copy-start.19
  687.2 4.5 copy-start.27
  695.5 38.0 %all-to-all-start.8 = ((bf16[3,512,256]{2,0,1:T(4,128)(2,1)}), bf16[3,512,256]{2,0,1:T(4,128)(2,1)}, u32[]{:S(2)}, u32[]{:S(2)}) async-start(bf16[3,512,256]{2,0,1:T(4,128)(2,1)} %pad_maximum_fusion), calls=%async_computation.8 | async-start | bytes 2097152 | tf_op jit(solution)/shard_map/all_to_all | solution.py:311
  699.8 1281.6 %all-reduce.7.cloned.1.call-start = ((), (), s32[]{:S(2)}) async-start(), calls=%async_computation.17 | async-start | bytes 67178496
  775.8 5.9 copy-start.10
  1008.8 1150.5 %all-reduce.5.cloned.1.call-start = ((), (), s32[]{:S(2)}) async-start(), calls=%async_computation.16 | async-start | bytes 8398848 | tf_op jit(solution)/shard_map/psum | solution.py:349
  2074.3 4.3 copy-start.14
  2185.7 11.2 copy-start.1
  (13 other events, 33.2 us)
Sparse Core Ops, SparseCore 0:
  10.7 101.4 all-gather.8
  114.8 97.5 all-gather.12
  214.6 46.1 all-gather.10
  262.7 47.7 all-gather.14
  312.4 124.1 all-gather.16
  438.7 122.6 all-gather.18
  1009.0 972.3 all-reduce.6
  2074.4 84.8 all-reduce.4
where the time goes:
time: 2220 us; the launch traced here: 2200 us
  waiting for transfers between devices  1400 us (63%)
  local copies, waits for them, and re-layouts  491 us (22%)
  matrix products  98.3 us (4%)
  blocking collectives  97.5 us (4%)
  starting transfers between devices  65.3 us (3%)
  other arithmetic  30.5 us (1%)
    unnamed x9, waiting for transfers between devices  974 us
    unnamed x118, local copies, waits for them, and re-layouts  285 us
    all_gather x1, waiting for transfers between devices, on_device(): lax.all_gather(ffn_in, 'dp', axis=0, tiled=True)  124 us
    all_gather x1, waiting for transfers between devices, on_device(): lax.all_gather(ffn_out, 'dp', axis=0, tiled=True)  120 us
    psum x1, waiting for transfers between devices, on_device(): summed = lax.psum(share, 'seq').astype(jnp.float32).reshape(seq_count, -1)  75.5 us
    all_gather x1, waiting for transfers between devices, on_device(): lax.all_gather(cross_qkv, 'dp', axis=1, tiled=True)  68.9 us
    convert_element_type x1, local copies, waits for them, and re-layouts, on_device(): grouped.astype(jnp.bfloat16)  59.6 us
    reshape x10, local copies, waits for them, and re-layouts, pack_grads(): blocks.append(moved.reshape(pieces, -1))  47.9 us
  transfers between devices with their start and end apart: 18, of which 9 were waited for; matrix products, arithmetic and copies ran while one was open for 7% of the time, Pallas kernels for 0%

commit v1 on v0

v1 whole, which is shorter than its diff:
```python
import functools
import types

import jax
import jax.numpy as jnp
from jax import lax
from jax.experimental import pallas as pl
from jax.experimental.pallas import tpu as pltpu
from jax.sharding import PartitionSpec as P

HD = 64
EPS = 1e-05
F32 = jnp.float32
BF = jnp.bfloat16
MESH = pl.DeviceIdType.MESH
ANY = pl.BlockSpec(memory_space=pl.ANY)
CH = 256
NS = 32
DP = "dp"
SEQ = "seq"
LO = "lo"
SMALL = "small"
LENS = "lens"
FIRST = "x"
FJ_MAX = 4096
AHEAD = 2
AHEAD_Y = 2
PLAN = (1, 1, 1, 1, 2, 1, 1, 1, 1, 1, 1, 0)
BPLAN = (0, 1, 1, 1, 0, 1, 2, 1, 1, 0, 1, 0, 1, 0, 1, 1, 1, 0, 1, 1)
PROBS = ("pbs", "pbc")


def configure(R, S, Tl, El, D, FF):
    g = types.SimpleNamespace(R=R, S=S, Tl=Tl, El=El, D=D, FF=FF)
    g.Y = 1
    while 8 * g.Y * g.Y <= R:
        g.Y *= 2
    g.Z = R // g.Y
    g.X = S // 2
    g.Dl = D // R
    g.FR = FF // R
    g.FB = g.FR // S
    g.DH = D // S
    g.FJ = FF // S
    g.NB = g.DH // 128
    g.H = g.DH // HD
    g.L = Tl * S
    g.E = El * S
    g.wide = g.Dl == 128 and g.FB == 128
    return g


def dot(a, b):
    return jnp.dot(a, b, preferred_element_type=F32)


def dot_nt(a, b):
    return lax.dot_general(a, b, (((1,), (1,)), ((), ())), preferred_element_type=F32)


def dot_tn(a, b):
    return lax.dot_general(a, b, (((0,), (0,)), ((), ())), preferred_element_type=F32)


def rem(a, b):
    return lax.rem(a, jnp.int32(b))


def at(start, size):
    if isinstance(start, int):
        return pl.ds(start, size)
    return pl.ds(pl.multiple_of(start, size), size)


def loop(count, body):
    if count == 1:
        body(0)
    else:
        lax.fori_loop(0, count, lambda n, z: (body(n), z)[1], 0)


def project(dst, a, w, transposed=False):
    def body(n):
        cols = at(n * 256, 256)
        dst[:, cols] = dot_nt(a, w[cols, :]) if transposed else dot(a, w[:, cols])

    loop(dst.shape[1] // 256, body)


def normalise(v):
    c = v - jnp.mean(v, axis=-1, keepdims=True)
    rstd = lax.rsqrt(jnp.mean(c * c, axis=-1, keepdims=True) + EPS)
    return c * rstd, rstd


class Comm:
    def __init__(self, g, r):
        self.g, self.r = g, r
        self.i = lax.axis_index(DP)
        self.j = lax.axis_index(SEQ)
        self.z, self.y = self.i // g.Y, rem(self.i, g.Y)
        self.x, self.c = self.j // 2, rem(self.j, 2)
        self.pending = []

    def zpeer(self, d):
        return (rem(self.z + d, self.g.Z) * self.g.Y + self.y, self.j)

    def ypeer(self, d):
        return (self.z * self.g.Y + rem(self.y + d, self.g.Y), self.j)

    def xpeer(self, d):
        return (self.i, rem(self.x + d, self.g.X) * 2 + self.c)

    def partner(self):
        return (self.i, self.x * 2 + 1 - self.c)

    def barrier(self):
        g = self.g
        peers = [self.zpeer(d) for d in range(1, g.Z)]
        peers += [self.ypeer(d) for d in range(1, g.Y)]
        peers += [self.xpeer(d) for d in range(1, g.X)]
        peers.append(self.partner())
        sem = pltpu.get_barrier_semaphore()
        for p in peers:
            pl.semaphore_signal(sem, inc=1, device_id=p, device_id_type=MESH)
        pl.semaphore_wait(sem, len(peers))

    def copy(self, src, dst, ss, rs, dev):
        return pltpu.make_async_remote_copy(
            src_ref=src, dst_ref=dst, send_sem=ss, recv_sem=rs, device_id=dev, device_id_type=MESH
        )

    def local(self, src, dst, sem):
        d = pltpu.make_async_copy(src, dst, sem)
        d.start()
        return d

    def when(self, cond, fn):
        if cond is None:
            fn()
        else:
            pl.when(cond)(fn)

    def w_descs(self, p, view, dz):
        r, g = self.r, self.g
        i = rem(self.z - dz + g.Z, g.Z) * g.Y + self.y
        v = view(i)
        return i, [
            self.copy(v, v, r.wys.at[p, d - 1, dz], r.wyr.at[p, d - 1, dz], self.ypeer(d))
            for d in range(1, g.Y)
        ]

    def w_z(self, p, view, d):
        v = view(self.i)
        r = self.r
        return self.copy(v, v, r.wzs.at[p, d - 1], r.wzr.at[p, d - 1], self.zpeer(d))

    def w_start(self, p, view, own=lambda i: None):
        def go():
            for d in range(1, self.g.Z):
                self.w_z(p, view, d).start()

        self.when(own(self.i), go)

    def w_relay(self, p, view, own=lambda i: None):
        r, g = self.r, self.g
        for dz in range(g.Z):
            i, descs = self.w_descs(p, view, dz)

            def go(i=i, descs=descs, dz=dz):
                v = view(i)
                if dz:
                    self.copy(
                        v, v, r.wzs.at[p, dz - 1], r.wzr.at[p, dz - 1], self.zpeer(dz)
                    ).wait_recv()
                for d in descs:
                    d.start()

            self.when(own(i), go)

    def w_finish(self, p, view, own=lambda i: None):
        r, g = self.r, self.g
        for dz in range(g.Z):
            for d in range(1, g.Y):
                i = rem(self.z - dz + g.Z, g.Z) * g.Y + rem(self.y - d + g.Y, g.Y)

                def go(i=i, d=d, dz=dz):
                    v = view(i)
                    self.copy(
                        v, v, r.wys.at[p, d - 1, dz], r.wyr.at[p, d - 1, dz], self.ypeer(d)
                    ).wait_recv()

                self.when(own(i), go)

    def w_drain(self, p, view, own=lambda i: None):
        g = self.g

        def go():
            for d in range(1, g.Z):
                self.w_z(p, view, d).wait_send()

        self.when(own(self.i), go)
        for dz in range(g.Z):
            i, descs = self.w_descs(p, view, dz)

            def go2(descs=descs):
                for d in descs:
                    d.wait_send()

            self.when(own(i), go2)

    def ag_x(self, k, view, d):
        v, r = view(self.j), self.r
        return self.copy(v, v, r.axs.at[k, d - 1], r.axr.at[k, d - 1], self.xpeer(d))

    def ag_c(self, k, view, d):
        g, r = self.g, self.r
        v = view(rem(self.x - d + g.X, g.X) * 2 + self.c)
        return self.copy(v, v, r.acs.at[k, d], r.acr.at[k, d], self.partner())

    def ag_start(self, k, view):
        for d in range(1, self.g.X):
            self.ag_x(k, view, d).start()
        self.ag_c(k, view, 0).start()

    def ag_relay(self, k, view):
        g, r = self.g, self.r
        for d in range(1, g.X):
            v = view(rem(self.x - d + g.X, g.X) * 2 + self.c)
            self.copy(
                v, v, r.axs.at[k, d - 1], r.axr.at[k, d - 1], self.xpeer(d)
            ).wait_recv()
            self.ag_c(k, view, d).start()

    def ag_finish(self, k, view):
        g, r = self.g, self.r
        for d in range(g.X):
            v = view(rem(self.x - d + g.X, g.X) * 2 + 1 - self.c)
            self.copy(v, v, r.acs.at[k, d], r.acr.at[k, d], self.partner()).wait_recv()

    def ag_drain(self, k, view):
        for d in range(1, self.g.X):
            self.ag_x(k, view, d).wait_send()
        for d in range(self.g.X):
            self.ag_c(k, view, d).wait_send()

    def rs_c(self, k, b, d):
        r = self.r
        return self.copy(
            b.ps.at[d], b.pr.at[d], r.rcs.at[k, d], r.rcr.at[k, d], self.partner()
        )

    def rs_x(self, k, b, d):
        r = self.r
        return self.copy(
            b.xs.at[d - 1],
            b.xr.at[d - 1],
            r.rxs.at[k, d - 1],
            r.rxr.at[k, d - 1],
            self.xpeer(d),
        )

    def rs_start(self, k, b, n, part):
        g = self.g
        for d in list(range(1, g.X)) + [0]:
            part(rem(self.x + d, g.X), b.part)
            b.acc[d] = b.part[at(self.c * n, n), :]
            b.ps[d] = b.part[at((1 - self.c) * n, n), :].astype(BF)
            self.rs_c(k, b, d).start()
        self.rs_turn(k, b)

    def rs_start_halves(self, k, b, n, part):
        g = self.g
        for d in list(range(1, g.X)) + [0]:
            first = rem(self.x + d, g.X) * 2 * n
            b.ps[d] = part(at(first + (1 - self.c) * n, n)).astype(BF)
            self.rs_c(k, b, d).start()
            b.acc[d] = part(at(first + self.c * n, n)).astype(b.acc.dtype)

    def rs_turn(self, k, b):
        for d in range(1, self.g.X):
            self.rs_c(k, b, d).wait_recv()
            b.xs[d - 1] = (b.acc[d][...].astype(F32) + b.pr[d].astype(F32)).astype(BF)
            self.rs_x(k, b, d).start()

    def rs_finish(self, k, b):
        g = self.g
        self.rs_c(k, b, 0).wait_recv()
        total = b.acc[0][...].astype(F32) + b.pr[0].astype(F32)
        for d in range(1, g.X):
            self.rs_x(k, b, d).wait_recv()
            total = total + b.xr[d - 1].astype(F32)
        for d in range(g.X):
            self.rs_c(k, b, d).wait_send()
        for d in range(1, g.X):
            self.rs_x(k, b, d).wait_send()
        return total

    def g_y(self, t, d, dz):
        g, r = self.g, self.r
        p, view, yr, zr, out = t
        i = rem(self.z + dz, g.Z) * g.Y + rem(self.y + d, g.Y)
        return self.copy(
            view(i),
            yr.at[d - 1, dz],
            r.gys.at[p, d - 1, dz],
            r.gyr.at[p, d - 1, dz],
            self.ypeer(d),
        )

    def g_z(self, t, dz):
        g, r = self.g, self.r
        p, view, yr, zr, out = t
        i = rem(self.z + dz, g.Z) * g.Y + self.y
        return self.copy(
            view(i), zr.at[dz - 1], r.gzs.at[p, dz - 1], r.gzr.at[p, dz - 1], self.zpeer(dz)
        )

    def g_start(self, t):
        for dz in list(range(1, self.g.Z)) + [0]:
            for d in range(1, self.g.Y):
                self.g_y(t, d, dz).start()

    def g_sum(self, t, dz):
        g = self.g
        p, view, yr, zr, out = t
        v = view(rem(self.z + dz, g.Z) * g.Y + self.y)
        total = v[...].astype(F32)
        for d in range(1, g.Y):
            self.g_y(t, d, dz).wait_recv()
            total = total + yr[d - 1, dz].astype(F32)
        return v, total

    def g_turn(self, t):
        for dz in range(1, self.g.Z):
            v, total = self.g_sum(t, dz)
            v[...] = total.astype(v.dtype)
            self.g_z(t, dz).start()

    def g_finish(self, t):
        p, view, yr, zr, out = t
        v, total = self.g_sum(t, 0)
        for dz in range(1, self.g.Z):
            self.g_z(t, dz).wait_recv()
            total = total + zr[dz - 1].astype(F32)
        out[...] = total.astype(out.dtype)

    def g_drain(self, t):
        for dz in range(self.g.Z):
            for d in range(1, self.g.Y):
                self.g_y(t, d, dz).wait_send()
        for dz in range(1, self.g.Z):
            self.g_z(t, dz).wait_send()


def attend_forward(g, q_ref, k_ref, v_ref, o_ref, p_ref, Lk, causal, limit, between):
    lane = lax.broadcasted_iota(jnp.int32, (1, 128), 1)
    low = lane < HD
    scale = HD ** -0.5
    for a in range(g.L // CH):
        rows = pl.ds(a * CH, CH)
        kk = (a + 1) * CH if causal else Lk
        keys = pl.ds(0, kk)
        col = lax.broadcasted_iota(jnp.int32, (CH, kk), 1)
        if causal:
            ok = col <= lax.broadcasted_iota(jnp.int32, (CH, kk), 0) + a * CH
        else:
            ok = col < limit

        def body(t):
            cols = at(t * 128, 128)
            q = q_ref[rows, cols]
            k = k_ref[keys, cols]
            v = v_ref[keys, cols]
            outs = []
            for e in range(2):
                qe = jnp.where(low if e == 0 else ~low, q, jnp.zeros_like(q))
                s = jnp.where(ok, dot_nt(qe, k) * scale, -1e30)
                ex = jnp.exp(s - jnp.max(s, axis=-1, keepdims=True))
                pb = (ex * (1.0 / jnp.sum(ex, axis=-1, keepdims=True))).astype(BF)
                p_ref[2 * t + e, rows, keys] = pb
                outs.append(dot(pb, v))
            o_ref[rows, cols] = jnp.where(low, outs[0], outs[1]).astype(BF)

        loop(g.NB, body)
        between(a)


def forward_kernel(g, names, *refs):
    r = types.SimpleNamespace(**dict(zip(names, refs)))
    cm = Comm(g, r)
    i, j, x, c = cm.i, cm.j, cm.x, cm.c
    Tl, El, D, Dl, DH, FB = g.Tl, g.El, g.D, g.Dl, g.DH, g.FB

    xv = lambda s: r.x.at[at(s * Tl, Tl), :]
    ev = lambda s: r.enc.at[at(s * El, El), :]
    lx = cm.local(r.tok, xv(j), r.ls.at[0])
    le = cm.local(r.states, ev(j), r.ls.at[1])

    own_rows = at(i * Dl, Dl)

    def col_block(t):
        return pl.ds(pl.multiple_of((t * g.S + j) * 128, 128), 128)

    def stage3(src, dst, sem):
        return [
            cm.local(
                src.at[:, :, col_block(t)], dst.at[:, own_rows, pl.ds(t * 128, 128)], sem.at[t]
            )
            for t in range(g.NB)
        ]

    def so_row(s):
        b = (s * Dl) // 128
        return (b // g.S) * 128 + rem(s * Dl, 128)

    def so_own(s):
        return rem((s * Dl) // 128, g.S) == j

    views = {}
    pieces = []

    def piece(view, own=lambda s: None):
        pieces.append((len(pieces), view, own))
        return pieces[-1]

    if g.wide:
        p_small = piece(lambda s: r.smalls.at[s])
    p_q = [piece(lambda s, n=n: r.wq.at[n, at(s * Dl, Dl), :]) for n in range(3)]
    p_so = piece(lambda s: r.wo.at[at(so_row(s), Dl), :], so_own)
    p_c = [piece(lambda s, n=n: r.wc.at[n, at(s * Dl, Dl), :]) for n in range(3)]
    p_co = piece(lambda s: r.wd.at[at(so_row(s), Dl), :], so_own)
    n1 = g.FJ // 256
    p_1 = [
        piece(lambda s, n=n: r.w1.at[at(s * Dl, Dl), pl.ds(n * 256, 256)]) for n in range(n1)
    ]
    n2 = D // 256
    p_2 = [
        piece(lambda s, n=n: r.w2.at[at(s * FB, FB), pl.ds(n * 256, 256)]) for n in range(n2)
    ]

    st_q = stage3(r.self_qkv, r.wq, r.lq)
    if g.wide:
        f = r.mine
        f[...] = jnp.zeros_like(f)
        nf = g.FF // D
        f[0:6, :] = r.attn_bias[...].astype(F32)
        f[6 : 6 + nf, :] = r.ffn_in_bias[...].astype(F32)
        f[6 + nf : 7 + nf, :] = r.ffn_out_bias[...].astype(F32)
        f[7 + nf : 10 + nf, :] = r.norm_gain[...].astype(F32)
        f[10 + nf : 13 + nf, :] = r.norm_bias[...].astype(F32)
        r.smalls[i] = f[...].astype(BF)

    def stage_row(src, dst, sem, wait):
        def go():
            d = pltpu.make_async_copy(src, dst.at[at(so_row(i), Dl), :], sem)
            if wait:
                d.wait()
            else:
                d.start()

        pl.when(so_own(i))(go)

    stage_row(r.self_out, r.wo, r.ls.at[3], False)
    st_c = stage3(r.cross_qkv, r.wc, r.lc)
    stage_row(r.cross_out, r.wd, r.ls.at[4], False)
    if g.wide:
        st_1 = [
            cm.local(
                r.ffn_in.at[:, pl.ds(pl.multiple_of((t * g.S + j) * 128, 128), 128)],
                r.w1.at[own_rows, pl.ds(t * 128, 128)],
                r.l1.at[t],
            )
            for t in range(g.R)
        ]
    else:
        st_1 = [cm.local(r.ffn_in, r.w1.at[own_rows, :], r.l1.at[0])]
    st_2 = [
        cm.local(r.ffn_out.at[at(j * FB, FB), :], r.w2.at[at(i * FB, FB), :], r.ls.at[5])
    ]

    cm.barrier()

    lx.wait()
    cm.ag_start(0, xv)
    staged = []
    for n in range(3):
        staged.append((p_q[n], st_q if n == 0 else [], None))
    staged.append((p_so, [], (r.self_out, r.wo, r.ls.at[3])))
    for n in range(3):
        staged.append((p_c[n], st_c if n == 0 else [], None))
    staged.append((p_co, [], (r.cross_out, r.wd, r.ls.at[4])))
    for n in range(n1):
        staged.append((p_1[n], st_1 if n == 0 else [], None))
    for n in range(n2):
        staged.append((p_2[n], st_2 if n == 0 else [], None))

    def start_next():
        if staged:
            p, descs, own_rows_copy = staged.pop(0)
            for d in descs:
                d.wait()
            if own_rows_copy:
                stage_row(*own_rows_copy, True)
            cm.w_start(*p)

    if g.wide:
        cm.w_start(*p_small)
    for _ in range(AHEAD):
        start_next()
    if g.wide:
        cm.w_relay(*p_small)
    cm.ag_relay(0, xv)
    le.wait()
    cm.ag_start(1, ev)
    for p in p_q:
        cm.w_relay(*p)
        start_next()
    cm.ag_relay(1, ev)
    cm.ag_finish(0, xv)
    if g.wide:
        cm.w_finish(*p_small)
        for s in range(g.R):
            r.sm[:, s * 128 : (s + 1) * 128] = r.smalls[s].astype(F32)
        r.fbv[0:1, :] = r.sm[pl.ds(6 + j, 1), :]
    else:
        r.sm[...] = r.small[...].astype(F32)
        r.fbv[0:1, :] = r.fbias[0:1, :]
    nb = 6 + g.FF // D

    outs = []

    def save(src, dst):
        outs.append(cm.local(src, dst, r.os.at[len(outs)]))

    def bias_cols(row):
        return jnp.concatenate([r.sm[row : row + 1, col_block(t)] for t in range(g.NB)], axis=1)

    def row_of(n):
        return r.sm[n : n + 1, :]

    queue = [p_so] + p_c + [p_co] + p_1 + p_2

    def relay(count):
        for _ in range(min(count, len(queue))):
            cm.w_relay(*queue.pop(0))
            start_next()

    plan = list(PLAN)

    zero = jnp.zeros((1, DH), F32)
    for n, v in enumerate((bias_cols(0), zero, bias_cols(1), zero, bias_cols(4), bias_cols(3))):
        r.bias[8 * n : 8 * n + 1, :] = v
    relay(plan[0])
    for p in p_q:
        cm.w_finish(*p)

    def qkv(n):
        r.qkv[n] = (dot(r.x[...], r.wq[n]) + r.bias[pl.ds(n * 8, 1), :]).astype(BF)

    loop(3, qkv)
    relay(plan[1])
    save(r.x, r.o_x)
    save(r.wq, r.o_wq)
    save(r.qkv, r.o_qkv)

    def between_self(a):
        relay(plan[2 + min(a, 1)])

    attend_forward(
        g,
        r.qkv.at[0],
        r.qkv.at[1],
        r.qkv.at[2],
        r.sof.at[j],
        r.pbs,
        g.L,
        True,
        None,
        between_self,
    )
    save(r.pbs, r.o_pbs)
    cm.w_finish(*p_so)
    save(r.wo, r.o_wo)

    buf = types.SimpleNamespace(part=r.part, acc=r.acc, ps=r.ps, pr=r.pr, xs=r.xs, xr=r.xr)

    def projected(src, w):
        def part(xx, dst):
            project(dst, src[at(xx * 2 * Tl, 2 * Tl), :], w)

        return part

    cm.rs_start(0, buf, Tl, projected(r.sof.at[j], r.wo))
    relay(plan[4])
    branch = cm.rs_finish(0, buf) + row_of(2)
    hat, rstd = normalise(xv(j)[...].astype(F32) + branch)
    r.h1[...] = hat
    r.rs1[...] = jnp.broadcast_to(rstd, (Tl, 128))
    first = hat * row_of(nb + 1) + row_of(nb + 4)
    r.res[...] = first
    fv = lambda s: r.fb.at[at(s * Tl, Tl), :]
    r.fb[at(j * Tl, Tl), :] = first.astype(BF)
    cm.ag_start(2, fv)
    save(r.h1, r.o_h1)
    save(r.rs1, r.o_rs1)

    cm.ag_finish(1, ev)
    relay(plan[5])
    for p in p_c:
        cm.w_finish(*p)

    def ckv(n):
        y = dot(r.enc[...], r.wc[n + 1]) + r.bias[pl.ds(n * 8 + 24, 1), :]
        r.ckv[n] = y.astype(BF)

    loop(2, ckv)
    save(r.enc, r.o_enc)
    save(r.ckv, r.o_ckv)
    cm.ag_relay(2, fv)
    save(r.wc, r.o_wc)
    cm.ag_finish(2, fv)
    r.cq[...] = (dot(r.fb[...], r.wc[0]) + r.bias[40:41, :]).astype(BF)
    save(r.fb, r.o_fb)
    save(r.cq, r.o_cq)

    sov = lambda s: r.sof.at[s]
    cov = lambda s: r.cof.at[s]
    cm.ag_start(4, sov)

    relay(plan[6])

    def between_cross(a):
        if a == 0:
            cm.ag_relay(4, sov)
        relay(plan[7 + min(a, 1)])

    attend_forward(
        g,
        r.cq,
        r.ckv.at[0],
        r.ckv.at[1],
        r.cof.at[j],
        r.pbc,
        g.E,
        False,
        r.lens[1],
        between_cross,
    )
    save(r.pbc, r.o_pbc)
    cm.w_finish(*p_co)
    save(r.wd, r.o_wd)
    cm.rs_start(1, buf, Tl, projected(r.cof.at[j], r.wd))
    relay(plan[9])
    branch = cm.rs_finish(1, buf) + row_of(5)
    hat, rstd = normalise(r.res[...] + branch)
    r.h2[...] = hat
    r.rs2[...] = jnp.broadcast_to(rstd, (Tl, 128))
    second = hat * row_of(nb + 2) + row_of(nb + 5)
    r.res[...] = second
    sv = lambda s: r.sb.at[at(s * Tl, Tl), :]
    r.sb[at(j * Tl, Tl), :] = second.astype(BF)
    cm.ag_start(3, sv)
    save(r.h2, r.o_h2)
    save(r.rs2, r.o_rs2)

    relay(plan[10])
    cm.ag_relay(3, sv)
    relay(plan[11])
    cm.ag_finish(3, sv)
    cm.ag_start(5, cov)
    cm.ag_finish(4, sov)
    save(r.sof, r.o_sof)
    while len(queue) > n2 or staged:
        relay(1)
    done = n2 - len(queue)
    first1, first2 = p_1[0][0], p_2[0][0]

    def piece1(n):
        return first1 + n, lambda s: r.w1.at[at(s * Dl, Dl), at(n * 256, 256)]

    def piece2(n):
        return first2 + n, lambda s: r.w2.at[at(s * FB, FB), at(n * 256, 256)]

    for p in queue[: len(queue) % n1]:
        cm.w_relay(*p)
        done += 1
    each = (n2 - done) // n1

    def hidden(n):
        cm.w_finish(*piece1(n))
        cols = at(n * 256, 256)
        pre = dot(r.sb[...], r.w1[:, cols]) + r.fbv[0:1, cols]
        cdf = 0.5 * (1.0 + lax.erf(pre * 0.7071067811865476))
        r.hid[:, cols] = (pre * cdf).astype(BF)
        r.dg[:, cols] = (cdf + pre * jnp.exp(-0.5 * pre * pre) * 0.3989422804014327).astype(BF)
        for e in range(each):
            cm.w_relay(*piece2(done + n * each + e))

    loop(n1, hidden)
    cm.ag_relay(5, cov)
    save(r.sb, r.o_sb)
    save(r.w1, r.o_w1)
    save(r.hid, r.o_hid)
    save(r.dg, r.o_dg)
    for p in p_2:
        cm.w_finish(*p)
    save(r.w2, r.o_w2)
    cm.rs_start(2, buf, Tl, projected(r.hid, r.w2))
    cm.ag_finish(5, cov)
    save(r.cof, r.o_cof)
    branch = cm.rs_finish(2, buf) + row_of(nb)
    hat, rstd = normalise(r.res[...] + branch)
    r.h3[...] = hat
    r.rs3[...] = jnp.broadcast_to(rstd, (Tl, 128))
    third = hat * row_of(nb + 3) + row_of(nb + 6)
    row = j * Tl + lax.broadcasted_iota(jnp.int32, (Tl, 1), 0)
    live = (row < r.lens[0]).astype(F32)
    r.lo[...] = (third * live).astype(BF)
    save(r.h3, r.o_h3)
    save(r.rs3, r.o_rs3)
    save(r.lo, r.o_lo)
    save(r.sm, r.o_sm)

    for p in pieces:
        cm.w_drain(*p)
    for k, v in enumerate((xv, ev, fv, sv, sov, cov)):
        cm.ag_drain(k, v)
    for d in outs:
        d.wait()


def forward_call(g, ins):
    names, in_specs, args = [], [], []
    for n, a in ins.items():
        names.append(n)
        args.append(a)
        if n == LENS:
            in_specs.append(pl.BlockSpec(memory_space=pltpu.SMEM))
        elif a.size <= 8 * FJ_MAX and n != LENS:
            in_specs.append(pl.BlockSpec(memory_space=pltpu.VMEM))
        else:
            in_specs.append(ANY)
    D, L, E, Tl = g.D, g.L, g.E, g.Tl
    keep = dict(
        x=((L, D), BF),
        enc=((E, D), BF),
        wq=((3, D, g.DH), BF),
        wo=((g.DH, D), BF),
        wc=((3, D, g.DH), BF),
        wd=((g.DH, D), BF),
        w1=((D, g.FJ), BF),
        w2=((g.FJ, D), BF),
        sm=((NS, D), F32),
        qkv=((3, L, g.DH), BF),
        sof=((g.S, L, g.DH), BF),
        pbs=((g.H, L, L), BF),
        fb=((L, D), BF),
        cq=((L, g.DH), BF),
        ckv=((2, E, g.DH), BF),
        cof=((g.S, L, g.DH), BF),
        pbc=((g.H, L, E), BF),
        sb=((L, D), BF),
        hid=((L, g.FJ), BF),
        dg=((L, g.FJ), BF),
        h1=((Tl, D), F32),
        h2=((Tl, D), F32),
        h3=((Tl, D), F32),
        rs1=((Tl, 128), F32),
        rs2=((Tl, 128), F32),
        rs3=((Tl, 128), F32),
        lo=((Tl, D), BF),
    )
    out_shape = [jax.ShapeDtypeStruct(*s) for s in keep.values()]
    names += ["o_" + n for n in keep]
    scratch = {n: pltpu.VMEM(*s) for n, s in keep.items()}
    scratch.update(res=pltpu.VMEM((Tl, D), F32))
    scratch.update(part=pltpu.VMEM((2 * Tl, D), F32))
    scratch.update(acc=pltpu.VMEM((g.X, Tl, D), F32))
    two = pltpu.VMEM((g.X, Tl, D), BF)
    one = pltpu.VMEM((g.X - 1, Tl, D), BF)
    scratch.update(ps=two, pr=two, xs=one, xr=one)
    if g.wide:
        scratch.update(smalls=pltpu.VMEM((g.R, NS, 128), BF), mine=pltpu.VMEM((NS, 128), F32))
    scratch.update(bias=pltpu.VMEM((48, g.DH), F32), fbv=pltpu.VMEM((8, g.FJ), F32))
    sem = pltpu.SemaphoreType.DMA
    NP = 9 + g.FJ // 256 + D // 256
    scratch.update(ls=sem((6,)))
    scratch.update(lq=sem((g.NB,)))
    scratch.update(lc=sem((g.NB,)))
    scratch.update(l1=sem((g.R,)))
    scratch.update(os=sem((len(keep),)))
    scratch.update(wzs=sem((NP, g.Z - 1)))
    scratch.update(wzr=sem((NP, g.Z - 1)))
    scratch.update(wys=sem((NP, g.Y - 1, g.Z)))
    scratch.update(wyr=sem((NP, g.Y - 1, g.Z)))
    scratch.update(axs=sem((6, g.X - 1)))
    scratch.update(axr=sem((6, g.X - 1)))
    scratch.update(acs=sem((6, g.X)))
    scratch.update(acr=sem((6, g.X)))
    scratch.update(rcs=sem((3, g.X)))
    scratch.update(rcr=sem((3, g.X)))
    scratch.update(rxs=sem((3, g.X - 1)))
    scratch.update(rxr=sem((3, g.X - 1)))
    names += list(scratch)
    out = pl.pallas_call(
        functools.partial(forward_kernel, g, names),
        out_shape=out_shape,
        in_specs=in_specs,
        out_specs=[ANY] * len(out_shape),
        scratch_shapes=list(scratch.values()),
        compiler_params=pltpu.CompilerParams(
            collective_id=0, has_side_effects=True, vmem_limit_bytes=60 << 20
        ),
    )(*args)
    return dict(zip(keep, out))


def attend_backward(g, q_ref, k_ref, v_ref, do_ref, src, bufs, outs, acc, Lk, causal, between):
    lane = lax.broadcasted_iota(jnp.int32, (1, 128), 1)
    low = lane < HD
    scale = HD ** -0.5
    dq_ref, dk_ref, dv_ref = outs
    dka, dva = acc
    pbuf, psem = bufs
    top = g.L // CH - 1

    def width(a):
        return (a + 1) * CH if causal else Lk

    def fetch(t, a, e):
        kk = width(a)
        return pltpu.make_async_copy(
            src.at[2 * t + e, pl.ds(a * CH, CH), pl.ds(0, kk)],
            pbuf.at[e, :, pl.ds(0, kk)],
            psem.at[e],
        )

    fetch(0, top, 0).start()
    for a in range(top, -1, -1):
        rows = pl.ds(a * CH, CH)
        kk = width(a)
        keys = pl.ds(0, kk)

        def body(t):
            cols = at(t * 128, 128)
            q = q_ref[rows, cols]
            do = do_ref[rows, cols]
            k = k_ref[keys, cols]
            v = v_ref[keys, cols]
            zero = jnp.zeros_like(q)
            dqs = []
            for e in range(2):
                fetch(t, a, e).wait()
                if e == 0:
                    fetch(t, a, 1).start()
                else:

                    @pl.when(t + 1 < g.NB)
                    def _():
                        fetch(t + 1, a, 0).start()

                    if a:

                        @pl.when(t + 1 == g.NB)
                        def _():
                            fetch(0, a - 1, 0).start()

                mine = low if e == 0 else ~low
                qe = jnp.where(mine, q, zero)
                doe = jnp.where(mine, do, zero)
                p = pbuf[e, :, keys]
                pf = p.astype(F32)
                w = dot_nt(doe, v) * pf
                ds = (w - pf * jnp.sum(w, axis=-1, keepdims=True)).astype(BF)
                dqs.append(dot(ds, k))
                dk = dot_tn(ds, qe)
                dv = dot_tn(p, doe)
                if a == top and e == 0:
                    dka[t, keys, :] = dk
                    dva[t, keys, :] = dv
                else:
                    dka[t, keys, :] += dk
                    dva[t, keys, :] += dv
            dq_ref[rows, cols] = (jnp.where(low, dqs[0], dqs[1]) * scale).astype(BF)

        loop(g.NB, body)
        between(a)

    def finish(t):
        cols = at(t * 128, 128)
        keys = pl.ds(0, Lk)
        dk_ref[keys, cols] = (dka[t, keys, :] * scale).astype(BF)
        dv_ref[keys, cols] = dva[t, keys, :].astype(BF)

    loop(g.NB, finish)


class Rows:
    def __init__(self, ref, first, size):
        self.ref, self.first, self.size, self.dtype = ref, first, size, ref.dtype
        self.at = self

    def rows(self, d):
        return pl.ds((self.first + d) * self.size, self.size)

    def __getitem__(self, d):
        return self.ref.at[self.rows(d), :]

    def __setitem__(self, d, value):
        self.ref[self.rows(d), :] = value


def colsum(v):
    return jnp.sum(v.astype(F32), axis=0, keepdims=True)


def backward_kernel(g, names, *refs):
    r = types.SimpleNamespace(**dict(zip(names, refs)))
    cm = Comm(g, r)
    i, j, c = cm.i, cm.j, cm.c
    Tl, El, D, Dl, DH, FB, FJ = g.Tl, g.El, g.D, g.Dl, g.DH, g.FB, g.FJ
    nb = 6 + g.FF // D

    loads = []

    def load(src, dst):
        loads.append(cm.local(src, dst, r.ls.at[len(loads)]))
        return loads[-1]

    l_og = load(r.i_og, r.og)
    l_h3 = load(r.i_h3, r.h3)
    l_rs3 = load(r.i_rs3, r.rs3)
    l_sm = load(r.i_sm, r.sm)
    l_w2 = load(r.i_w2, r.w2)
    l_dg = load(r.i_dg, r.dg)
    l_w1 = load(r.i_w1, r.w1)
    l_hid = load(r.i_hid, r.hid)
    l_sb = load(r.i_sb, r.sb)
    l_h2 = load(r.i_h2, r.h2)
    l_rs2 = load(r.i_rs2, r.rs2)
    l_wd = load(r.i_wd, r.wd)
    l_cof = load(r.i_cof, r.cof)
    l_ckv = load(r.i_ckv, r.ckv)
    l_cq = load(r.i_cq, r.cq)
    l_wc = load(r.i_wc, r.wc)
    l_fb = load(r.i_fb, r.fb)
    l_enc = load(r.i_enc, r.enc)
    l_h1 = load(r.i_h1, r.h1)
    l_rs1 = load(r.i_rs1, r.rs1)
    l_wo = load(r.i_wo, r.wo)
    l_qkv = load(r.i_qkv, r.qkv)
    l_sof = load(r.i_sof, r.sof)
    l_wq = load(r.i_wq, r.wq)

    cm.barrier()
    r.sg[...] = jnp.zeros_like(r.sg)

    def col_block(t):
        return pl.ds(pl.multiple_of((t * g.S + j) * 128, 128), 128)

    def put_cols(row, value):
        for t in range(g.NB):
            r.sg[row : row + 1, col_block(t)] = value[:, t * 128 : (t + 1) * 128]

    own = at(j * Tl, Tl)

    def norm_back(gr, hat, rstd, n):
        r.sg[nb + 1 + n : nb + 2 + n, :] = jnp.sum(gr * hat, axis=0, keepdims=True)
        r.sg[nb + 4 + n : nb + 5 + n, :] = jnp.sum(gr, axis=0, keepdims=True)
        gn = gr * r.sm[nb + 1 + n : nb + 2 + n, :]
        return rstd[:, 0:1] * (
            gn
            - jnp.mean(gn, axis=-1, keepdims=True)
            - hat * jnp.mean(gn * hat, axis=-1, keepdims=True)
        )

    def send_dy(k, dh, buf, bias_row):
        low = dh.astype(BF)
        buf[own, :] = low
        view = lambda s: buf.at[at(s * Tl, Tl), :]
        cm.ag_start(k, view)
        r.sg[bias_row : bias_row + 1, :] = colsum(low)
        return view

    n1 = FJ // 256
    n2 = D // 256
    tasks = []

    def task(view, yr, zr, out):
        tasks.append((len(tasks), view, yr, zr, out))
        return tasks[-1]

    t_2 = [
        task(
            lambda s, n=n: r.d2.at[at(s * FB, FB), pl.ds(n * 256, 256)],
            r.yr2.at[n],
            r.zr2.at[n],
            r.g2.at[j, :, pl.ds(n * 256, 256)],
        )
        for n in range(n2)
    ]
    t_1 = [
        task(
            lambda s, n=n: r.d1.at[at(s * Dl, Dl), pl.ds(n * 256, 256)],
            r.yr1.at[n],
            r.zr1.at[n],
            r.g1.at[j, :, pl.ds(n * 256, 256)],
        )
        for n in range(n1)
    ]
    t_c = [
        task(
            lambda s, n=n: r.dc.at[n, at(s * Dl, Dl), :], r.yrc.at[n], r.zrc.at[n], r.gc.at[j, n]
        )
        for n in range(4)
    ]
    t_s = [
        task(
            lambda s, n=n: r.ds.at[n, at(s * Dl, Dl), :], r.yrs.at[n], r.zrs.at[n], r.gs.at[j, n]
        )
        for n in range(4)
    ]
    if g.wide:
        t_g = task(
            lambda s: r.sg.at[:, pl.ds(pl.multiple_of(s * 128, 128), 128)],
            r.yrg,
            r.zrg,
            r.gg.at[j],
        )
    waiting, turns, ends = [], [], []

    def pump():
        while waiting and len(turns) < AHEAD_Y:
            t = waiting.pop(0)
            cm.g_start(t)
            turns.append(t)

    def launch(*ts):
        waiting.extend(ts)
        pump()

    def turn(count):
        for _ in range(min(count, len(turns) + len(waiting))):
            t = turns.pop(0)
            cm.g_turn(t)
            ends.append(t)
            pump()

    def complete(group):
        for t in group:
            while t not in ends:
                turn(1)
            cm.g_finish(t)
            ends.remove(t)

    points = list(BPLAN)

    def point():
        turn(points.pop(0) if points else 0)

    outs = []
    outs2 = []
    finals = []

    def save(src, dst):
        outs.append(cm.local(src, dst, r.os.at[len(outs)]))

    def save_2(s):
        return [(r.g2.at[s], r.o_f2.at[at(s * FB, FB), :])]

    def save_1(s):
        if not g.wide:
            return [(r.g1.at[s], r.o_f1.at[s])]
        return [
            (r.g1.at[s, :, pl.ds(t * 128, 128)], r.o_f1.at[:, at((t * g.S + s) * 128, 128)])
            for t in range(g.R)
        ]

    def save_n(src, d3, d1, parts=range(4)):
        def pairs(s):
            res = []
            for t in range(g.NB):
                cols = at((t * g.S + s) * 128, 128)
                mine = pl.ds(t * 128, 128)
                for n in parts:
                    dst = d3.at[n, :, cols] if n < 3 else d1.at[:, cols]
                    res.append((src.at[s, n, :, mine], dst))
            return res

        return pairs

    def gather(k, view, pairs):
        cm.ag_start(k, view)
        finals.append((k, view, pairs))

    def flush():
        for k, view, pairs in finals:
            cm.ag_finish(k, view)
            todo = [pair for s in range(g.S) for pair in pairs(s)]
            for n, (src, dst) in enumerate(todo):
                outs2.append(cm.local(src, dst, r.fs.at[k - 3, n]))

    for d in (l_og, l_h3, l_rs3, l_sm):
        d.wait()
    row = j * Tl + lax.broadcasted_iota(jnp.int32, (Tl, 1), 0)
    live = (row < r.lens[0]).astype(F32)
    g3 = r.og[...].astype(F32) * live
    dh3 = norm_back(g3, r.h3[...], r.rs3[...], 2)
    r.dh[...] = dh3
    v3 = send_dy(0, dh3, r.dya, nb)

    for d in (l_w2, l_dg, l_hid):
        d.wait()
    cm.ag_relay(0, v3)
    cm.ag_finish(0, v3)

    def grad_2(n):
        cols = at(n * 256, 256)
        r.d2[:, cols] = dot_tn(r.hid[...], r.dya[:, cols]).astype(BF)

    def hidden_back(n):
        cols = at(n * 256, 256)
        y = dot_nt(r.dya[...], r.w2[cols, :]) * r.dg[:, cols].astype(F32)
        y = y.astype(BF)
        r.dpre[:, cols] = y
        r.fsum[0:1, cols] = colsum(y)

    grad_2(0)
    launch(t_2[0])
    loop(n2 - 1, lambda n: grad_2(n + 1))
    launch(*t_2[1:])
    loop(n1, hidden_back)
    point()
    if g.wide:
        r.sg[pl.ds(6 + j, 1), :] = r.fsum[0:1, :]
    else:
        r.fg[...] = r.fsum[...]
    l_w1.wait()

    def part3(xx, dst):
        project(dst, r.dpre[at(xx * 2 * Tl, 2 * Tl), :], r.w1, True)

    buf = types.SimpleNamespace(part=r.part, acc=r.acc, ps=r.ps, pr=r.pr, xs=r.xs, xr=r.xr)
    cm.rs_start(0, buf, Tl, part3)
    l_sb.wait()
    point()

    def grad_1(n):
        cols = at(n * 256, 256)
        r.d1[:, cols] = dot_tn(r.sb[...], r.dpre[:, cols]).astype(BF)

    loop(n1, grad_1)
    l_x = load(r.i_x, r.sb)
    launch(*t_1)
    for d in (l_h2, l_rs2):
        d.wait()
    point()
    dh2 = norm_back(r.dh[...] + cm.rs_finish(0, buf), r.h2[...], r.rs2[...], 1)
    r.dh[...] = dh2
    v2 = send_dy(1, dh2, r.dyb, 5)
    for d in (l_wd, l_ckv, l_cq):
        d.wait()
    point()
    cm.ag_relay(1, v2)
    point()

    cm.ag_finish(1, v2)
    r.do[...] = dot_nt(r.dyb[...], r.wd[...]).astype(BF)
    point()

    def between_cross(a):
        point()

    attend_backward(
        g,
        r.cq,
        r.ckv.at[0],
        r.ckv.at[1],
        r.do,
        r.i_pbc,
        (r.pbuf, r.psem),
        (r.dcq, r.dckv.at[0], r.dckv.at[1]),
        (r.dka, r.dva),
        g.E,
        False,
        between_cross,
    )
    l_wc.wait()

    def part4(xx, dst):
        project(dst, r.dcq[at(xx * 2 * Tl, 2 * Tl), :], r.wc.at[0], True)

    cm.ag_drain(0, v3)
    cm.rs_start(1, buf, Tl, part4)
    point()
    put_cols(3, colsum(r.dcq[...]))
    put_cols(4, colsum(r.dckv[1]))
    for d in (l_fb, l_h1, l_rs1, l_enc):
        d.wait()

    def grad_rows(dst, a, b):
        def body(n):
            rows = at(n * 256, 256)
            dst[rows, :] = dot_tn(a[:, rows], b[...]).astype(BF)

        loop(D // 256, body)

    grad_rows(r.dc.at[1], r.enc, r.dckv.at[0])
    launch(t_c[1])
    point()
    dh1 = norm_back(r.dh[...] + cm.rs_finish(1, buf), r.h1[...], r.rs1[...], 0)
    r.dh[...] = dh1
    v1 = send_dy(2, dh1, r.dya, 2)
    point()
    grad_rows(r.dc.at[2], r.enc, r.dckv.at[1])
    launch(t_c[2])
    point()
    cm.ag_relay(2, v1)
    grad_rows(r.dc.at[0], r.fb, r.dcq)
    launch(t_c[0])
    point()
    complete(t_2)
    gather(3, lambda s: r.g2.at[s], save_2)
    ebuf = types.SimpleNamespace(
        acc=Rows(r.enc, 0, El), ps=Rows(r.enc, g.X, El), pr=r.epr, xs=r.exs, xr=r.exr
    )

    def part_e(rows):
        return dot_nt(r.dckv[0, rows, :], r.wc[1]) + dot_nt(r.dckv[1, rows, :], r.wc[2])

    def grad_out(full, dy, dst):
        dyj = jnp.concatenate([dy[:, col_block(t)] for t in range(g.NB)], axis=1)

        def body(s):
            y = dot_tn(full[s], dyj).astype(BF)
            for t in range(g.NB):
                dst[at((t * g.S + s) * 128, 128), :] = y[t * 128 : (t + 1) * 128, :]

        loop(g.S, body)

    for d in (l_wo, l_qkv, l_cof, l_sof):
        d.wait()
    grad_out(r.cof, r.dyb, r.dc.at[3])
    launch(t_c[3])
    point()

    cm.ag_finish(2, v1)
    r.do[...] = dot_nt(r.dya[...], r.wo[...]).astype(BF)
    grad_out(r.sof, r.dya, r.ds.at[3])
    launch(t_s[3])
    point()
    cm.rs_start_halves(3, ebuf, El, part_e)
    complete(t_1)
    gather(4, lambda s: r.g1.at[s], save_1)

    def between_self(a):
        if a == g.L // CH - 1:
            cm.ag_relay(*finals[0][:2])
            cm.rs_turn(3, ebuf)
        point()

    attend_backward(
        g,
        r.qkv.at[0],
        r.qkv.at[1],
        r.qkv.at[2],
        r.do,
        r.i_pbs,
        (r.pbuf, r.psem),
        (r.dqkv.at[0], r.dqkv.at[1], r.dqkv.at[2]),
        (r.dka, r.dva),
        g.L,
        True,
        between_self,
    )
    for d in (l_wq, l_x):
        d.wait()

    def part5(xx, dst):
        rows = at(xx * 2 * Tl, 2 * Tl)

        def body(n):
            cols = at(n * 256, 256)
            dst[:, cols] = (
                dot_nt(r.dqkv[0, rows, :], r.wq[0, cols, :])
                + dot_nt(r.dqkv[1, rows, :], r.wq[1, cols, :])
                + dot_nt(r.dqkv[2, rows, :], r.wq[2, cols, :])
            )

        loop(D // 256, body)

    put_cols(0, colsum(r.dqkv[0]))
    put_cols(1, colsum(r.dqkv[2]))
    if g.wide:
        launch(t_g)
    for n in range(3):
        grad_rows(r.ds.at[n], r.sb, r.dqkv.at[n])
        launch(t_s[n])
        point()
    cm.rs_start(2, buf, Tl, part5)
    cm.ag_relay(*finals[1][:2])
    complete(t_c)
    gather(5, lambda s: r.gc.at[s], save_n(r.gc, r.o_cq, r.o_co))
    r.ge[...] = cm.rs_finish(3, ebuf).astype(BF)
    save(r.ge, r.o_ge)
    r.gi[...] = (r.dh[...] + cm.rs_finish(2, buf)).astype(BF)
    save(r.gi, r.o_gi)
    order = [3, 0, 1, 2]
    for m, n in enumerate(order):
        complete([t_s[n]])
        gather(6 + n, lambda s, n=n: r.gs.at[s, n], save_n(r.gs, r.o_sq, r.o_so, [n]))
        cm.ag_relay(*finals[m + 2][:2])
        if n == 3 and g.wide:
            complete([t_g])
            cm.ag_start(10, lambda s: r.gg.at[s])
    cm.ag_relay(*finals[6][:2])
    v_gg = lambda s: r.gg.at[s]
    if g.wide:
        cm.ag_relay(10, v_gg)
        cm.ag_finish(10, v_gg)
    flush()
    if g.wide:
        total = r.gg[0]
        for s in range(1, g.S):
            total = total + r.gg[s]
        r.gsum[...] = total
        save(r.gsum, r.o_small)
    else:
        save(r.sg, r.o_small)
        save(r.fg, r.o_fg)

    cm.ag_drain(1, v2)
    cm.ag_drain(2, v1)
    for k, view, pairs in finals:
        cm.ag_drain(k, view)
    if g.wide:
        cm.ag_drain(10, v_gg)
    for t in tasks:
        cm.g_drain(t)
    for d in outs + outs2:
        d.wait()


def backward_call(g, lens, out_grad, f):
    D, L, E, Tl, El, S = g.D, g.L, g.E, g.Tl, g.El, g.S
    Dl, DH, FJ, FB = g.Dl, g.DH, g.FJ, g.FB
    loaded = [n for n in f if n not in PROBS and n != FIRST]
    names = ["lens", "i_og"] + ["i_" + n for n in f]
    args = [lens, out_grad] + list(f.values())
    in_specs = [pl.BlockSpec(memory_space=pltpu.SMEM)] + [ANY] * (len(args) - 1)
    V = pltpu.VMEM
    scratch = {n: V(f[n].shape, f[n].dtype) for n in loaded}
    small = (NS, 128) if g.wide else (NS, D)
    outs = dict(
        gi=((Tl, D), BF),
        ge=((El, D), BF),
        f2=((g.FR, D), BF),
        f1=((Dl, g.FF) if g.wide else (S, Dl, FJ), BF),
        cq=((3, Dl, D), BF),
        co=((Dl, D), BF),
        sq=((3, Dl, D), BF),
        so=((Dl, D), BF),
        small=(small, F32),
    )
    if not g.wide:
        outs.update(fg=((8, FJ), F32))
        scratch.update(fg=V((8, FJ), F32))
    names += ["o_" + n for n in outs]
    scratch.update(
        gi=V((Tl, D), BF),
        ge=V((El, D), BF),
        g2=V((S, FB, D), BF),
        g1=V((S, Dl, FJ), BF),
        gc=V((S, 4, Dl, DH), BF),
        gs=V((S, 4, Dl, DH), BF),
        fsum=V((8, FJ), F32),
    )
    two = V((g.X, Tl, D), BF)
    one = V((g.X - 1, Tl, D), BF)
    scratch.update(
        og=V((Tl, D), BF),
        dh=V((Tl, D), F32),
        sg=V((NS, D), F32),
        part=V((2 * Tl, D), F32),
        acc=V((g.X, Tl, D), F32),
        ps=two,
        pr=two,
        xs=one,
        xr=one,
        epr=V((g.X, El, D), BF),
        exs=V((g.X - 1, El, D), BF),
        exr=V((g.X - 1, El, D), BF),
        dya=V((L, D), BF),
        dyb=V((L, D), BF),
        dpre=V((L, FJ), BF),
        do=V((L, DH), BF),
        dcq=V((L, DH), BF),
        dckv=V((2, E, DH), BF),
        dqkv=V((3, L, DH), BF),
        dka=V((g.NB, E, 128), F32),
        dva=V((g.NB, E, 128), F32),
        pbuf=V((2, CH, E), BF),
        d2=V((FJ, D), BF),
        d1=V((D, FJ), BF),
        dc=V((4, D, DH), BF),
        ds=V((4, D, DH), BF),
        yr2=V((D // 256, g.Y - 1, g.Z, FB, 256), BF),
        yr1=V((FJ // 256, g.Y - 1, g.Z, Dl, 256), BF),
        yrc=V((4, g.Y - 1, g.Z, Dl, DH), BF),
        yrs=V((4, g.Y - 1, g.Z, Dl, DH), BF),
        zr2=V((D // 256, g.Z - 1, FB, 256), BF),
        zr1=V((FJ // 256, g.Z - 1, Dl, 256), BF),
        zrc=V((4, g.Z - 1, Dl, DH), BF),
        zrs=V((4, g.Z - 1, Dl, DH), BF),
    )
    if g.wide:
        scratch.update(
            yrg=V((g.Y - 1, g.Z, NS, 128), F32),
            zrg=V((g.Z - 1, NS, 128), F32),
            gg=V((S, NS, 128), F32),
            gsum=V((NS, 128), F32),
        )
    sem = pltpu.SemaphoreType.DMA
    NP = 9 + FJ // 256 + D // 256
    scratch.update(
        ls=sem((26,)),
        os=sem((8,)),
        psem=sem((2,)),
        fs=sem((7, max(S * (g.R if g.wide else 1), 4 * S * g.NB))),
        gys=sem((NP, g.Y - 1, g.Z)),
        gyr=sem((NP, g.Y - 1, g.Z)),
        gzs=sem((NP, g.Z - 1)),
        gzr=sem((NP, g.Z - 1)),
        axs=sem((11, g.X - 1)),
        axr=sem((11, g.X - 1)),
        acs=sem((11, g.X)),
        acr=sem((11, g.X)),
        rcs=sem((4, g.X)),
        rcr=sem((4, g.X)),
        rxs=sem((4, g.X - 1)),
        rxr=sem((4, g.X - 1)),
    )
    names += list(scratch)
    out = pl.pallas_call(
        functools.partial(backward_kernel, g, names),
        out_shape=[jax.ShapeDtypeStruct(*s) for s in outs.values()],
        in_specs=in_specs,
        out_specs=[ANY] * len(outs),
        scratch_shapes=list(scratch.values()),
        compiler_params=pltpu.CompilerParams(
            collective_id=1, has_side_effects=True, vmem_limit_bytes=67043328
        ),
    )(*args)
    return dict(zip(outs, out))


def finish_kernel(cuts, *refs):
    half = (len(refs) - len(cuts)) // 2
    ins, small = refs[:half], refs[half]
    outs, smalls = refs[half + 1 : 2 * half + 1], refs[2 * half + 1 :]
    for src, dst in zip(ins, outs):
        dst[...] = src[...].astype(dst.dtype)
    for (lo, hi), dst in zip(cuts, smalls):
        dst[...] = small[lo:hi, :]


def finish_call(g, parts, small):
    steps = 4 if g.Dl % 64 == 0 else 2
    nf = g.FF // g.D
    cuts = ((0, 6), (6, 6 + nf), (6 + nf, 7 + nf), (7 + nf, 10 + nf), (10 + nf, 13 + nf))
    specs, shapes = [], []
    for n, (a, dtype) in enumerate(parts):
        block = list(a.shape)
        block[-2] //= steps
        lead = a.ndim - 2
        specs.append(pl.BlockSpec(tuple(block), lambda k, lead=lead: (0,) * lead + (k, 0)))
        shapes.append(jax.ShapeDtypeStruct(a.shape, dtype))
    for lo, hi in cuts:
        shapes.append(jax.ShapeDtypeStruct((hi - lo, small.shape[1]), F32))

    def whole(shape):
        return pl.BlockSpec(shape, lambda k: (0, 0))

    return pl.pallas_call(
        functools.partial(finish_kernel, cuts),
        grid=(steps,),
        out_shape=shapes,
        in_specs=specs + [whole(small.shape)],
        out_specs=specs + [whole(s.shape) for s in shapes[len(specs) :]],
        compiler_params=pltpu.CompilerParams(vmem_limit_bytes=67043328),
    )(*[a for a, _ in parts], small)


def on_device(
    decoder_in,
    encoder_states,
    out_grad,
    seq_lengths,
    enc_lengths,
    self_qkv,
    self_out,
    cross_qkv,
    cross_out,
    attn_bias,
    ffn_in,
    ffn_in_bias,
    ffn_out,
    ffn_out_bias,
    norm_gain,
    norm_bias,
):
    R = lax.axis_size(DP)
    S = lax.axis_size(SEQ)
    j = lax.axis_index(SEQ)
    D = decoder_in.shape[2]
    FF = ffn_in.shape[1]
    g = configure(R, S, decoder_in.shape[1], encoder_states.shape[1], D, FF)
    Dl, FR, FB, FJ, NB = g.Dl, g.FR, g.FB, g.FJ, g.NB
    nf = FF // D
    nb = 6 + nf

    fi, fo = ffn_in_bias.reshape(nf, Dl), ffn_out_bias.reshape(1, Dl)
    lens = jnp.concatenate([seq_lengths, enc_lengths])
    ins = dict(
        lens=lens,
        tok=decoder_in[0],
        states=encoder_states[0],
        self_qkv=self_qkv,
        self_out=self_out,
        cross_qkv=cross_qkv,
        cross_out=cross_out,
        ffn_in=ffn_in,
        ffn_out=ffn_out,
    )
    if g.wide:
        ins.update(
            attn_bias=attn_bias,
            ffn_in_bias=fi,
            ffn_out_bias=fo,
            norm_gain=norm_gain,
            norm_bias=norm_bias,
        )
    else:
        pad = jnp.zeros((NS - nb - 7, Dl), BF)
        small = jnp.concatenate([attn_bias, fi, fo, norm_gain, norm_bias, pad])
        small = lax.all_gather(small, DP, axis=1, tiled=True)
        fb = small[6:nb].reshape(nf, R, Dl).transpose(1, 0, 2)
        fb = lax.dynamic_slice_in_dim(fb.reshape(R, FR), j * FB, FB, axis=1).reshape(1, -1)
        packed = lax.dynamic_slice_in_dim(ffn_in.reshape(Dl, R, FR), j * FB, FB, axis=2)
        ins.update(
            small=small,
            fbias=jnp.broadcast_to(fb.astype(F32), (8, FJ)),
            ffn_in=packed.reshape(Dl, FJ),
        )
    f = forward_call(g, ins)
    lo = f.pop(LO)
    b = types.SimpleNamespace(**backward_call(g, lens, out_grad[0], f))

    sm = b.small
    if not g.wide:
        fpl = lax.dynamic_update_slice(
            jnp.zeros((R, S, FB), F32), b.fg[0].reshape(R, 1, FB), (0, j, 0)
        )
        fpl = fpl.reshape(R, nf, Dl).transpose(1, 0, 2).reshape(nf, D)
        sm = lax.dynamic_update_slice(sm, fpl, (6, 0))
        sm = lax.psum(lax.psum_scatter(sm, DP, scatter_dimension=1, tiled=True), SEQ)

    gw1 = b.f1
    if not g.wide:
        gw1 = gw1.reshape(S, Dl, R, FB).transpose(1, 2, 0, 3).reshape(Dl, FF)
    parts = [(lo, BF), (b.gi, BF), (b.ge, BF)]
    parts += [(a, F32) for a in (b.sq, b.so, b.cq, b.co, gw1, b.f2)]
    lo, gi, ge, sq, so, cq, co, f1, f2, gab, gfi, gfo, ggain, gshift = finish_call(g, parts, sm)
    return (
        lo[None],
        gi[None],
        ge[None],
        sq,
        so,
        cq,
        co,
        gab,
        f1,
        gfi.reshape(-1),
        f2,
        gfo.reshape(-1),
        ggain,
        gshift,
    )


def solution(mesh):
    act = P(DP, SEQ, None)
    w3 = P(None, DP, None)
    w2 = P(DP, None)
    v2 = P(None, DP)
    v1 = P(DP)
    return jax.shard_map(
        on_device,
        mesh=mesh,
        in_specs=(act, act, act, v1, v1, w3, w2, w3, w2, v2, w2, v1, w2, v1, v2, v2),
        out_specs=(act, act, act, w3, w2, w3, w2, v2, w2, v1, w2, v1, v2, v2),
        check_vma=False,
    )
```

time: 2220 us -> 278 us (0.13)
  waiting for transfers between devices: 1400 us -> 0 us
  local copies, waits for them, and re-layouts: 491 us -> 0 us
  Pallas kernels: 0 us -> 274 us
  matrix products: 98.3 us -> 0 us
  blocking collectives: 97.5 us -> 0 us
  starting transfers between devices: 65.3 us -> 0 us
  other arithmetic: 30.5 us -> 0.59 us
    unnamed x9 -> x0, waiting for transfers between devices: 974 us -> none
    all_gather x6 -> x0, waiting for transfers between devices: 347 us -> none  [the longest x1 124 us: on_device(): lax.all_gather(ffn_in, 'dp', axis=0, tiled=True)]
    unnamed x118 -> x0, local copies, waits for them, and re-layouts: 285 us -> none
    pallas_call x0 -> x3, Pallas kernels: none -> 274 us  [the longest x1 146 us: backward_call(): pl.pallas_call(functools.partial(backward_kernel, g, names), out_shape=[j...]
    dot_general x33 -> x0, matrix products: 98.3 us -> none  [the longest x2 8.32 us: one_step(): jnp.einsum('qhd,khd->hqk', do_block, values3, preferred_element_type=jnp....]
    all_gather x5 -> x0, blocking collectives: 97.5 us -> none  [the longest x1 26 us: on_device(): lax.all_gather(attn_bias, 'dp', axis=1, tiled=True)]
    psum x1 -> x0, waiting for transfers between devices: 75.5 us -> none  [on_device(): summed = lax.psum(share, 'seq').astype(jnp.float32).reshape(seq_count, -1)]
    reshape x22 -> x0, local copies, waits for them, and re-layouts: 74 us -> none  [the longest x10 47.9 us: pack_grads(): blocks.append(moved.reshape(pieces, -1))]
  transfers between devices with their start and end apart: 18 -> 0, of which waited for: 9 -> 0; matrix products, arithmetic and copies ran while one was open for 7% -> 0% of each run, Pallas kernels for 0% -> 0%
where the time goes in v1:
time: 278 us; the launch traced here: 277 us
  Pallas kernels  274 us (99%)
    pallas_call x1, Pallas kernels, backward_call(): pl.pallas_call(functools.partial(backward_kernel, g, names), out_shape=[j...  146 us
    pallas_call x1, Pallas kernels, forward_call(): pl.pallas_call(functools.partial(forward_kernel, g, names), out_shape=out...  122 us
    pallas_call x1, Pallas kernels, finish_call(): pl.pallas_call(functools.partial(finish_kernel, cuts), grid=(steps,), out...  6.4 us

profile of v1, /device:TPU:1, one launch (start us, length us, event | category | flops | bytes accessed | tf_op | source)
XLA Modules:
  0.0 276.8 jit_solution(13962940268971550927)
XLA Ops:
  1.9 0.6 pad_add_fusion.refs_0_
  2.5 121.8 %shard_map.263 = (bf16[512,1024]{1,0:T(8,128)(2,1)}, bf16[1024,1024]{1,0:T(8,128)(2,1)}, bf16[3,1024,256]{2,1,0:T(8,128)(2,1)}, bf16[256,1024]{1,0:T(8,128)(2,1)...) custom-call(s32[2]{0:T(128)} %pad_add_fusion.refs_0_, ...), custom_call_target="tpu_custom_call" | custom-call | tf_op jit(solution)/shard_map/pallas_call | solution.py:806
  124.3 145.9 %shard_map.264 = (bf16[128,1024]{1,0:T(8,128)(2,1)}, bf16[256,1024]{1,0:T(8,128)(2,1)}, bf16[512,1024]{1,0:T(8,128)(2,1)}, bf16[128,4096]{1,0:T(8,128)(2,1)}, bf...) custom-call(s32[2]{0:T(128)} %pad_add_fusion.refs_0_, ...), custom_call_target="tpu_custom_call" | custom-call | tf_op jit(solution)/shard_map/pallas_call | solution.py:1445
  270.2 6.4 %shard_map.265 = (bf16[128,1024]{1,0:T(8,128)(2,1)}, bf16[128,1024]{1,0:T(8,128)(2,1)}, bf16[256,1024]{1,0:T(8,128)(2,1)}, f32[3,128,1024]{2,1,0:T(8,128)}, f32[...) custom-call(bf16[128,1024]{1,0:T(8,128)(2,1)} %get-tuple-element.64., ...), custom_call_target="tpu_custom_call" | custom-call | tf_op jit(solution)/shard_map/pallas_call | solution.py:1485

commit v2 on v1

--- a/solution.py
+++ b/solution.py
@@ -18,16 +18,12 @@
 NS = 32
 DP = "dp"
 SEQ = "seq"
-LO = "lo"
-SMALL = "small"
 LENS = "lens"
-FIRST = "x"
 FJ_MAX = 4096
 AHEAD = 2
 AHEAD_Y = 2
-PLAN = (1, 1, 1, 1, 2, 1, 1, 1, 1, 1, 1, 0)
+PLAN = (1, 1, 1, 1, 2, 1, 1, 1, 1, 1, 1, 0, 1)
 BPLAN = (0, 1, 1, 1, 0, 1, 2, 1, 1, 0, 1, 0, 1, 0, 1, 1, 1, 0, 1, 1)
-PROBS = ("pbs", "pbc")
 
 
 def configure(R, S, Tl, El, D, FF):
@@ -94,8 +90,8 @@
 
 
 class Comm:
-    def __init__(self, g, r):
-        self.g, self.r = g, r
+    def __init__(self, g, r, ka=0, kr=0):
+        self.g, self.r, self.ka, self.kr = g, r, ka, kr
         self.i = lax.axis_index(DP)
         self.j = lax.axis_index(SEQ)
         self.z, self.y = self.i // g.Y, rem(self.i, g.Y)
@@ -211,12 +207,12 @@
 
     def ag_x(self, k, view, d):
         v, r = view(self.j), self.r
-        return self.copy(v, v, r.axs.at[k, d - 1], r.axr.at[k, d - 1], self.xpeer(d))
+        return self.copy(v, v, r.axs.at[self.ka + k, d - 1], r.axr.at[self.ka + k, d - 1], self.xpeer(d))
 
     def ag_c(self, k, view, d):
         g, r = self.g, self.r
         v = view(rem(self.x - d + g.X, g.X) * 2 + self.c)
-        return self.copy(v, v, r.acs.at[k, d], r.acr.at[k, d], self.partner())
+        return self.copy(v, v, r.acs.at[self.ka + k, d], r.acr.at[self.ka + k, d], self.partner())
 
     def ag_start(self, k, view):
         for d in range(1, self.g.X):
@@ -228,7 +224,7 @@
         for d in range(1, g.X):
             v = view(rem(self.x - d + g.X, g.X) * 2 + self.c)
             self.copy(
-                v, v, r.axs.at[k, d - 1], r.axr.at[k, d - 1], self.xpeer(d)
+                v, v, r.axs.at[self.ka + k, d - 1], r.axr.at[self.ka + k, d - 1], self.xpeer(d)
             ).wait_recv()
             self.ag_c(k, view, d).start()
 
@@ -236,7 +232,7 @@
         g, r = self.g, self.r
         for d in range(g.X):
             v = view(rem(self.x - d + g.X, g.X) * 2 + 1 - self.c)
-            self.copy(v, v, r.acs.at[k, d], r.acr.at[k, d], self.partner()).wait_recv()
+            self.copy(v, v, r.acs.at[self.ka + k, d], r.acr.at[self.ka + k, d], self.partner()).wait_recv()
 
     def ag_drain(self, k, view):
         for d in range(1, self.g.X):
@@ -244,21 +240,19 @@
         for d in range(self.g.X):
             self.ag_c(k, view, d).wait_send()
 
-    def rs_c(self, k, b, d):
-        r = self.r
-        return self.copy(
-            b.ps.at[d], b.pr.at[d], r.rcs.at[k, d], r.rcr.at[k, d], self.partner()
-        )
-
-    def rs_x(self, k, b, d):
-        r = self.r
-        return self.copy(
-            b.xs.at[d - 1],
-            b.xr.at[d - 1],
-            r.rxs.at[k, d - 1],
-            r.rxr.at[k, d - 1],
-            self.xpeer(d),
-        )
+    def rs_c(self, k, b, d, cols=None):
+        r, k = self.r, k + self.kr
+        src, dst = b.ps.at[d], b.pr.at[d]
+        if cols is not None:
+            src, dst = src.at[:, cols], dst.at[:, cols]
+        return self.copy(src, dst, r.rcs.at[k, d], r.rcr.at[k, d], self.partner())
+
+    def rs_x(self, k, b, d, cols=None):
+        r, k = self.r, k + self.kr
+        src, dst = b.xs.at[d - 1], b.xr.at[d - 1]
+        if cols is not None:
+            src, dst = src.at[:, cols], dst.at[:, cols]
+        return self.copy(src, dst, r.rxs.at[k, d - 1], r.rxr.at[k, d - 1], self.xpeer(d))
 
     def rs_start(self, k, b, n, part):
         g = self.g
@@ -277,23 +271,29 @@
             self.rs_c(k, b, d).start()
             b.acc[d] = part(at(first + self.c * n, n)).astype(b.acc.dtype)
 
-    def rs_turn(self, k, b):
+    def rs_turn(self, k, b, cols=None):
         for d in range(1, self.g.X):
-            self.rs_c(k, b, d).wait_recv()
-            b.xs[d - 1] = (b.acc[d][...].astype(F32) + b.pr[d].astype(F32)).astype(BF)
-            self.rs_x(k, b, d).start()
-
-    def rs_finish(self, k, b):
+            self.rs_c(k, b, d, cols).wait_recv()
+            if cols is None:
+                b.xs[d - 1] = (b.acc[d][...].astype(F32) + b.pr[d].astype(F32)).astype(BF)
+            else:
+                total = b.acc[d, :, cols].astype(F32) + b.pr[d, :, cols].astype(F32)
+                b.xs[d - 1, :, cols] = total.astype(BF)
+            self.rs_x(k, b, d, cols).start()
+
+    def rs_finish(self, k, b, cols=None):
         g = self.g
-        self.rs_c(k, b, 0).wait_recv()
-        total = b.acc[0][...].astype(F32) + b.pr[0].astype(F32)
+        here = pl.ds(0, g.D) if cols is None else cols
+        self.rs_c(k, b, 0, cols).wait_recv()
+        own = b.acc[0][...] if cols is None else b.acc[0, :, cols]
+        total = own.astype(F32) + b.pr[0, :, here].astype(F32)
         for d in range(1, g.X):
-            self.rs_x(k, b, d).wait_recv()
-            total = total + b.xr[d - 1].astype(F32)
+            self.rs_x(k, b, d, cols).wait_recv()
+            total = total + b.xr[d - 1, :, here].astype(F32)
         for d in range(g.X):
-            self.rs_c(k, b, d).wait_send()
+            self.rs_c(k, b, d, cols).wait_send()
         for d in range(1, g.X):
-            self.rs_x(k, b, d).wait_send()
+            self.rs_x(k, b, d, cols).wait_send()
         return total
 
     def g_y(self, t, d, dz):
@@ -353,10 +353,20 @@
             self.g_z(t, dz).wait_send()
 
 
-def attend_forward(g, q_ref, k_ref, v_ref, o_ref, p_ref, Lk, causal, limit, between):
+def attend_forward(g, q_ref, k_ref, v_ref, o_ref, dst, bufs, Lk, causal, limit, between):
     lane = lax.broadcasted_iota(jnp.int32, (1, 128), 1)
     low = lane < HD
     scale = HD ** -0.5
+    pbuf, psem = bufs
+
+    def put(t, a, e):
+        keys = pl.ds(0, (a + 1) * CH if causal else Lk)
+        return pltpu.make_async_copy(
+            pbuf.at[2 * t + e, :, keys],
+            dst.at[2 * t + e, pl.ds(a * CH, CH), keys],
+            psem.at[2 * t + e],
+        )
+
     for a in range(g.L // CH):
         rows = pl.ds(a * CH, CH)
         kk = (a + 1) * CH if causal else Lk
@@ -378,19 +388,24 @@
                 s = jnp.where(ok, dot_nt(qe, k) * scale, -1e30)
                 ex = jnp.exp(s - jnp.max(s, axis=-1, keepdims=True))
                 pb = (ex * (1.0 / jnp.sum(ex, axis=-1, keepdims=True))).astype(BF)
-                p_ref[2 * t + e, rows, keys] = pb
+                if a:
+                    put(t, a - 1, e).wait()
+                pbuf[2 * t + e, :, keys] = pb
+                put(t, a, e).start()
                 outs.append(dot(pb, v))
             o_ref[rows, cols] = jnp.where(low, outs[0], outs[1]).astype(BF)
 
         loop(g.NB, body)
         between(a)
-
-
-def forward_kernel(g, names, *refs):
-    r = types.SimpleNamespace(**dict(zip(names, refs)))
-    cm = Comm(g, r)
+    for t in range(g.NB):
+        for e in range(2):
+            put(t, g.L // CH - 1, e).wait()
+
+
+def forward_body(g, r, cm, state):
     i, j, x, c = cm.i, cm.j, cm.x, cm.c
     Tl, El, D, Dl, DH, FB = g.Tl, g.El, g.D, g.Dl, g.DH, g.FB
+    state.l_og = cm.local(r.out_grad, r.og, r.ls.at[6])
 
     xv = lambda s: r.x.at[at(s * Tl, Tl), :]
     ev = lambda s: r.enc.at[at(s * El, El), :]
@@ -480,6 +495,7 @@
     ]
 
     cm.barrier()
+    r.sg[...] = jnp.zeros_like(r.sg)
 
     lx.wait()
     cm.ag_start(0, xv)
@@ -528,11 +544,6 @@
         r.fbv[0:1, :] = r.fbias[0:1, :]
     nb = 6 + g.FF // D
 
-    outs = []
-
-    def save(src, dst):
-        outs.append(cm.local(src, dst, r.os.at[len(outs)]))
-
     def bias_cols(row):
         return jnp.concatenate([r.sm[row : row + 1, col_block(t)] for t in range(g.NB)], axis=1)
 
@@ -560,9 +571,7 @@
 
     loop(3, qkv)
     relay(plan[1])
-    save(r.x, r.o_x)
-    save(r.wq, r.o_wq)
-    save(r.qkv, r.o_qkv)
+    save_x = cm.local(r.x, r.o_x, r.ls.at[7])
 
     def between_self(a):
         relay(plan[2 + min(a, 1)])
@@ -573,15 +582,14 @@
         r.qkv.at[1],
         r.qkv.at[2],
         r.sof.at[j],
-        r.pbs,
+        r.o_pbs,
+        (r.pbuf, r.psem),
         g.L,
         True,
         None,
         between_self,
     )
-    save(r.pbs, r.o_pbs)
     cm.w_finish(*p_so)
-    save(r.wo, r.o_wo)
 
     buf = types.SimpleNamespace(part=r.part, acc=r.acc, ps=r.ps, pr=r.pr, xs=r.xs, xr=r.xr)
 
@@ -598,12 +606,10 @@
     r.h1[...] = hat
     r.rs1[...] = jnp.broadcast_to(rstd, (Tl, 128))
     first = hat * row_of(nb + 1) + row_of(nb + 4)
-    r.res[...] = first
+    r.dh[...] = first
     fv = lambda s: r.fb.at[at(s * Tl, Tl), :]
     r.fb[at(j * Tl, Tl), :] = first.astype(BF)
     cm.ag_start(2, fv)
-    save(r.h1, r.o_h1)
-    save(r.rs1, r.o_rs1)
 
     cm.ag_finish(1, ev)
     relay(plan[5])
@@ -615,14 +621,9 @@
         r.ckv[n] = y.astype(BF)
 
     loop(2, ckv)
-    save(r.enc, r.o_enc)
-    save(r.ckv, r.o_ckv)
     cm.ag_relay(2, fv)
-    save(r.wc, r.o_wc)
     cm.ag_finish(2, fv)
     r.cq[...] = (dot(r.fb[...], r.wc[0]) + r.bias[40:41, :]).astype(BF)
-    save(r.fb, r.o_fb)
-    save(r.cq, r.o_cq)
 
     sov = lambda s: r.sof.at[s]
     cov = lambda s: r.cof.at[s]
@@ -641,28 +642,27 @@
         r.ckv.at[0],
         r.ckv.at[1],
         r.cof.at[j],
-        r.pbc,
+        r.o_pbc,
+        (r.pbuf, r.psem),
         g.E,
         False,
         r.lens[1],
         between_cross,
     )
-    save(r.pbc, r.o_pbc)
     cm.w_finish(*p_co)
-    save(r.wd, r.o_wd)
+    save_x.wait()
+    cm.ag_drain(0, xv)
     cm.rs_start(1, buf, Tl, projected(r.cof.at[j], r.wd))
     relay(plan[9])
     branch = cm.rs_finish(1, buf) + row_of(5)
-    hat, rstd = normalise(r.res[...] + branch)
+    hat, rstd = normalise(r.dh[...] + branch)
     r.h2[...] = hat
     r.rs2[...] = jnp.broadcast_to(rstd, (Tl, 128))
     second = hat * row_of(nb + 2) + row_of(nb + 5)
-    r.res[...] = second
-    sv = lambda s: r.sb.at[at(s * Tl, Tl), :]
-    r.sb[at(j * Tl, Tl), :] = second.astype(BF)
+    r.dh[...] = second
+    sv = lambda s: r.x.at[at(s * Tl, Tl), :]
+    r.x[at(j * Tl, Tl), :] = second.astype(BF)
     cm.ag_start(3, sv)
-    save(r.h2, r.o_h2)
-    save(r.rs2, r.o_rs2)
 
     relay(plan[10])
     cm.ag_relay(3, sv)
@@ -670,150 +670,51 @@
     cm.ag_finish(3, sv)
     cm.ag_start(5, cov)
     cm.ag_finish(4, sov)
-    save(r.sof, r.o_sof)
     while len(queue) > n2 or staged:
         relay(1)
-    done = n2 - len(queue)
-    first1, first2 = p_1[0][0], p_2[0][0]
+    first1 = p_1[0][0]
 
     def piece1(n):
         return first1 + n, lambda s: r.w1.at[at(s * Dl, Dl), at(n * 256, 256)]
-
-    def piece2(n):
-        return first2 + n, lambda s: r.w2.at[at(s * FB, FB), at(n * 256, 256)]
-
-    for p in queue[: len(queue) % n1]:
-        cm.w_relay(*p)
-        done += 1
-    each = (n2 - done) // n1
 
     def hidden(n):
         cm.w_finish(*piece1(n))
         cols = at(n * 256, 256)
-        pre = dot(r.sb[...], r.w1[:, cols]) + r.fbv[0:1, cols]
+        pre = dot(r.x[...], r.w1[:, cols]) + r.fbv[0:1, cols]
         cdf = 0.5 * (1.0 + lax.erf(pre * 0.7071067811865476))
         r.hid[:, cols] = (pre * cdf).astype(BF)
         r.dg[:, cols] = (cdf + pre * jnp.exp(-0.5 * pre * pre) * 0.3989422804014327).astype(BF)
-        for e in range(each):
-            cm.w_relay(*piece2(done + n * each + e))
-
-    loop(n1, hidden)
+
+    half = n1 // 2
+    loop(half, hidden)
+    relay(plan[12])
+    loop(n1 - half, lambda n: hidden(n + half))
     cm.ag_relay(5, cov)
-    save(r.sb, r.o_sb)
-    save(r.w1, r.o_w1)
-    save(r.hid, r.o_hid)
-    save(r.dg, r.o_dg)
+    relay(len(queue))
     for p in p_2:
         cm.w_finish(*p)
-    save(r.w2, r.o_w2)
     cm.rs_start(2, buf, Tl, projected(r.hid, r.w2))
     cm.ag_finish(5, cov)
-    save(r.cof, r.o_cof)
     branch = cm.rs_finish(2, buf) + row_of(nb)
-    hat, rstd = normalise(r.res[...] + branch)
+    hat, rstd = normalise(r.dh[...] + branch)
     r.h3[...] = hat
     r.rs3[...] = jnp.broadcast_to(rstd, (Tl, 128))
     third = hat * row_of(nb + 3) + row_of(nb + 6)
     row = j * Tl + lax.broadcasted_iota(jnp.int32, (Tl, 1), 0)
     live = (row < r.lens[0]).astype(F32)
     r.lo[...] = (third * live).astype(BF)
-    save(r.h3, r.o_h3)
-    save(r.rs3, r.o_rs3)
-    save(r.lo, r.o_lo)
-    save(r.sm, r.o_sm)
-
-    for p in pieces:
-        cm.w_drain(*p)
-    for k, v in enumerate((xv, ev, fv, sv, sov, cov)):
-        cm.ag_drain(k, v)
-    for d in outs:
-        d.wait()
-
-
-def forward_call(g, ins):
-    names, in_specs, args = [], [], []
-    for n, a in ins.items():
-        names.append(n)
-        args.append(a)
-        if n == LENS:
-            in_specs.append(pl.BlockSpec(memory_space=pltpu.SMEM))
-        elif a.size <= 8 * FJ_MAX and n != LENS:
-            in_specs.append(pl.BlockSpec(memory_space=pltpu.VMEM))
-        else:
-            in_specs.append(ANY)
-    D, L, E, Tl = g.D, g.L, g.E, g.Tl
-    keep = dict(
-        x=((L, D), BF),
-        enc=((E, D), BF),
-        wq=((3, D, g.DH), BF),
-        wo=((g.DH, D), BF),
-        wc=((3, D, g.DH), BF),
-        wd=((g.DH, D), BF),
-        w1=((D, g.FJ), BF),
-        w2=((g.FJ, D), BF),
-        sm=((NS, D), F32),
-        qkv=((3, L, g.DH), BF),
-        sof=((g.S, L, g.DH), BF),
-        pbs=((g.H, L, L), BF),
-        fb=((L, D), BF),
-        cq=((L, g.DH), BF),
-        ckv=((2, E, g.DH), BF),
-        cof=((g.S, L, g.DH), BF),
-        pbc=((g.H, L, E), BF),
-        sb=((L, D), BF),
-        hid=((L, g.FJ), BF),
-        dg=((L, g.FJ), BF),
-        h1=((Tl, D), F32),
-        h2=((Tl, D), F32),
-        h3=((Tl, D), F32),
-        rs1=((Tl, 128), F32),
-        rs2=((Tl, 128), F32),
-        rs3=((Tl, 128), F32),
-        lo=((Tl, D), BF),
-    )
-    out_shape = [jax.ShapeDtypeStruct(*s) for s in keep.values()]
-    names += ["o_" + n for n in keep]
-    scratch = {n: pltpu.VMEM(*s) for n, s in keep.items()}
-    scratch.update(res=pltpu.VMEM((Tl, D), F32))
-    scratch.update(part=pltpu.VMEM((2 * Tl, D), F32))
-    scratch.update(acc=pltpu.VMEM((g.X, Tl, D), F32))
-    two = pltpu.VMEM((g.X, Tl, D), BF)
-    one = pltpu.VMEM((g.X - 1, Tl, D), BF)
-    scratch.update(ps=two, pr=two, xs=one, xr=one)
-    if g.wide:
-        scratch.update(smalls=pltpu.VMEM((g.R, NS, 128), BF), mine=pltpu.VMEM((NS, 128), F32))
-    scratch.update(bias=pltpu.VMEM((48, g.DH), F32), fbv=pltpu.VMEM((8, g.FJ), F32))
-    sem = pltpu.SemaphoreType.DMA
-    NP = 9 + g.FJ // 256 + D // 256
-    scratch.update(ls=sem((6,)))
-    scratch.update(lq=sem((g.NB,)))
-    scratch.update(lc=sem((g.NB,)))
-    scratch.update(l1=sem((g.R,)))
-    scratch.update(os=sem((len(keep),)))
-    scratch.update(wzs=sem((NP, g.Z - 1)))
-    scratch.update(wzr=sem((NP, g.Z - 1)))
-    scratch.update(wys=sem((NP, g.Y - 1, g.Z)))
-    scratch.update(wyr=sem((NP, g.Y - 1, g.Z)))
-    scratch.update(axs=sem((6, g.X - 1)))
-    scratch.update(axr=sem((6, g.X - 1)))
-    scratch.update(acs=sem((6, g.X)))
-    scratch.update(acr=sem((6, g.X)))
-    scratch.update(rcs=sem((3, g.X)))
-    scratch.update(rcr=sem((3, g.X)))
-    scratch.update(rxs=sem((3, g.X - 1)))
-    scratch.update(rxr=sem((3, g.X - 1)))
-    names += list(scratch)
-    out = pl.pallas_call(
-        functools.partial(forward_kernel, g, names),
-        out_shape=out_shape,
-        in_specs=in_specs,
-        out_specs=[ANY] * len(out_shape),
-        scratch_shapes=list(scratch.values()),
-        compiler_params=pltpu.CompilerParams(
-            collective_id=0, has_side_effects=True, vmem_limit_bytes=60 << 20
-        ),
-    )(*args)
-    return dict(zip(keep, out))
+    state.outs.append(cm.local(r.lo, r.o_lo, r.ls.at[8]))
+
+    def drain():
+        for p in pieces:
+            cm.w_drain(*p)
+        for k, v in ((2, fv), (4, sov), (5, cov)):
+            cm.ag_drain(k, v)
+
+    state.drain = drain
+    state.drain_second = lambda: cm.ag_drain(3, sv)
+    state.drain_states = lambda: cm.ag_drain(1, ev)
+    state.live = live
 
 
 def attend_backward(g, q_ref, k_ref, v_ref, do_ref, src, bufs, outs, acc, Lk, causal, between):
@@ -832,11 +733,13 @@
         kk = width(a)
         return pltpu.make_async_copy(
             src.at[2 * t + e, pl.ds(a * CH, CH), pl.ds(0, kk)],
-            pbuf.at[e, :, pl.ds(0, kk)],
-            psem.at[e],
+            pbuf.at[2 * t + e, :, pl.ds(0, kk)],
+            psem.at[2 * t + e],
         )
 
-    fetch(0, top, 0).start()
+    for t in range(g.NB):
+        for e in range(2):
+            fetch(t, top, e).start()
     for a in range(top, -1, -1):
         rows = pl.ds(a * CH, CH)
         kk = width(a)
@@ -852,30 +755,18 @@
             dqs = []
             for e in range(2):
                 fetch(t, a, e).wait()
-                if e == 0:
-                    fetch(t, a, 1).start()
-                else:
-
-                    @pl.when(t + 1 < g.NB)
-                    def _():
-                        fetch(t + 1, a, 0).start()
-
-                    if a:
-
-                        @pl.when(t + 1 == g.NB)
-                        def _():
-                            fetch(0, a - 1, 0).start()
-
                 mine = low if e == 0 else ~low
                 qe = jnp.where(mine, q, zero)
                 doe = jnp.where(mine, do, zero)
-                p = pbuf[e, :, keys]
+                p = pbuf[2 * t + e, :, keys]
                 pf = p.astype(F32)
                 w = dot_nt(doe, v) * pf
                 ds = (w - pf * jnp.sum(w, axis=-1, keepdims=True)).astype(BF)
                 dqs.append(dot(ds, k))
                 dk = dot_tn(ds, qe)
                 dv = dot_tn(p, doe)
+                if a:
+                    fetch(t, a - 1, e).start()
                 if a == top and e == 0:
                     dka[t, keys, :] = dk
                     dva[t, keys, :] = dv
@@ -915,46 +806,10 @@
     return jnp.sum(v.astype(F32), axis=0, keepdims=True)
 
 
-def backward_kernel(g, names, *refs):
-    r = types.SimpleNamespace(**dict(zip(names, refs)))
-    cm = Comm(g, r)
+def backward_body(g, r, cm, state):
     i, j, c = cm.i, cm.j, cm.c
     Tl, El, D, Dl, DH, FB, FJ = g.Tl, g.El, g.D, g.Dl, g.DH, g.FB, g.FJ
     nb = 6 + g.FF // D
-
-    loads = []
-
-    def load(src, dst):
-        loads.append(cm.local(src, dst, r.ls.at[len(loads)]))
-        return loads[-1]
-
-    l_og = load(r.i_og, r.og)
-    l_h3 = load(r.i_h3, r.h3)
-    l_rs3 = load(r.i_rs3, r.rs3)
-    l_sm = load(r.i_sm, r.sm)
-    l_w2 = load(r.i_w2, r.w2)
-    l_dg = load(r.i_dg, r.dg)
-    l_w1 = load(r.i_w1, r.w1)
-    l_hid = load(r.i_hid, r.hid)
-    l_sb = load(r.i_sb, r.sb)
-    l_h2 = load(r.i_h2, r.h2)
-    l_rs2 = load(r.i_rs2, r.rs2)
-    l_wd = load(r.i_wd, r.wd)
-    l_cof = load(r.i_cof, r.cof)
-    l_ckv = load(r.i_ckv, r.ckv)
-    l_cq = load(r.i_cq, r.cq)
-    l_wc = load(r.i_wc, r.wc)
-    l_fb = load(r.i_fb, r.fb)
-    l_enc = load(r.i_enc, r.enc)
-    l_h1 = load(r.i_h1, r.h1)
-    l_rs1 = load(r.i_rs1, r.rs1)
-    l_wo = load(r.i_wo, r.wo)
-    l_qkv = load(r.i_qkv, r.qkv)
-    l_sof = load(r.i_sof, r.sof)
-    l_wq = load(r.i_wq, r.wq)
-
-    cm.barrier()
-    r.sg[...] = jnp.zeros_like(r.sg)
 
     def col_block(t):
         return pl.ds(pl.multiple_of((t * g.S + j) * 128, 128), 128)
@@ -1059,7 +914,7 @@
     def point():
         turn(points.pop(0) if points else 0)
 
-    outs = []
+    outs = state.outs
     outs2 = []
     finals = []
 
@@ -1101,17 +956,12 @@
             for n, (src, dst) in enumerate(todo):
                 outs2.append(cm.local(src, dst, r.fs.at[k - 3, n]))
 
-    for d in (l_og, l_h3, l_rs3, l_sm):
-        d.wait()
-    row = j * Tl + lax.broadcasted_iota(jnp.int32, (Tl, 1), 0)
-    live = (row < r.lens[0]).astype(F32)
-    g3 = r.og[...].astype(F32) * live
+    state.l_og.wait()
+    g3 = r.og[...].astype(F32) * state.live
     dh3 = norm_back(g3, r.h3[...], r.rs3[...], 2)
     r.dh[...] = dh3
     v3 = send_dy(0, dh3, r.dya, nb)
 
-    for d in (l_w2, l_dg, l_hid):
-        d.wait()
     cm.ag_relay(0, v3)
     cm.ag_finish(0, v3)
 
@@ -1136,31 +986,26 @@
         r.sg[pl.ds(6 + j, 1), :] = r.fsum[0:1, :]
     else:
         r.fg[...] = r.fsum[...]
-    l_w1.wait()
 
     def part3(xx, dst):
         project(dst, r.dpre[at(xx * 2 * Tl, 2 * Tl), :], r.w1, True)
 
     buf = types.SimpleNamespace(part=r.part, acc=r.acc, ps=r.ps, pr=r.pr, xs=r.xs, xr=r.xr)
     cm.rs_start(0, buf, Tl, part3)
-    l_sb.wait()
     point()
 
     def grad_1(n):
         cols = at(n * 256, 256)
-        r.d1[:, cols] = dot_tn(r.sb[...], r.dpre[:, cols]).astype(BF)
+        r.d1[:, cols] = dot_tn(r.x[...], r.dpre[:, cols]).astype(BF)
 
     loop(n1, grad_1)
-    l_x = load(r.i_x, r.sb)
+    state.drain_second()
+    l_x = cm.local(r.o_x, r.x, r.ls.at[9])
     launch(*t_1)
-    for d in (l_h2, l_rs2):
-        d.wait()
     point()
     dh2 = norm_back(r.dh[...] + cm.rs_finish(0, buf), r.h2[...], r.rs2[...], 1)
     r.dh[...] = dh2
     v2 = send_dy(1, dh2, r.dyb, 5)
-    for d in (l_wd, l_ckv, l_cq):
-        d.wait()
     point()
     cm.ag_relay(1, v2)
     point()
@@ -1178,7 +1023,7 @@
         r.ckv.at[0],
         r.ckv.at[1],
         r.do,
-        r.i_pbc,
+        r.o_pbc,
         (r.pbuf, r.psem),
         (r.dcq, r.dckv.at[0], r.dckv.at[1]),
         (r.dka, r.dva),
@@ -1186,7 +1031,6 @@
         False,
         between_cross,
     )
-    l_wc.wait()
 
     def part4(xx, dst):
         project(dst, r.dcq[at(xx * 2 * Tl, 2 * Tl), :], r.wc.at[0], True)
@@ -1196,8 +1040,6 @@
     point()
     put_cols(3, colsum(r.dcq[...]))
     put_cols(4, colsum(r.dckv[1]))
-    for d in (l_fb, l_h1, l_rs1, l_enc):
-        d.wait()
 
     def grad_rows(dst, a, b):
         def body(n):
@@ -1206,6 +1048,18 @@
 
         loop(D // 256, body)
 
+    def grad_out(full, dy, dst):
+        dyj = jnp.concatenate([dy[:, col_block(t)] for t in range(g.NB)], axis=1)
+
+        def body(s):
+            y = dot_tn(full[s], dyj).astype(BF)
+            for t in range(g.NB):
+                dst[at((t * g.S + s) * 128, 128), :] = y[t * 128 : (t + 1) * 128, :]
+
+        loop(g.S, body)
+
+    grad_out(r.cof, r.dyb, r.dc.at[3])
+    launch(t_c[3])
     grad_rows(r.dc.at[1], r.enc, r.dckv.at[0])
     launch(t_c[1])
     point()
@@ -1229,20 +1083,6 @@
     def part_e(rows):
         return dot_nt(r.dckv[0, rows, :], r.wc[1]) + dot_nt(r.dckv[1, rows, :], r.wc[2])
 
-    def grad_out(full, dy, dst):
-        dyj = jnp.concatenate([dy[:, col_block(t)] for t in range(g.NB)], axis=1)
-
-        def body(s):
-            y = dot_tn(full[s], dyj).astype(BF)
-            for t in range(g.NB):
-                dst[at((t * g.S + s) * 128, 128), :] = y[t * 128 : (t + 1) * 128, :]
-
-        loop(g.S, body)
-
-    for d in (l_wo, l_qkv, l_cof, l_sof):
-        d.wait()
-    grad_out(r.cof, r.dyb, r.dc.at[3])
-    launch(t_c[3])
     point()
 
     cm.ag_finish(2, v1)
@@ -1250,6 +1090,7 @@
     grad_out(r.sof, r.dya, r.ds.at[3])
     launch(t_s[3])
     point()
+    state.drain_states()
     cm.rs_start_halves(3, ebuf, El, part_e)
     complete(t_1)
     gather(4, lambda s: r.g1.at[s], save_1)
@@ -1266,7 +1107,7 @@
         r.qkv.at[1],
         r.qkv.at[2],
         r.do,
-        r.i_pbs,
+        r.o_pbs,
         (r.pbuf, r.psem),
         (r.dqkv.at[0], r.dqkv.at[1], r.dqkv.at[2]),
         (r.dka, r.dva),
@@ -1274,8 +1115,6 @@
         True,
         between_self,
     )
-    for d in (l_wq, l_x):
-        d.wait()
 
     def part5(xx, dst):
         rows = at(xx * 2 * Tl, 2 * Tl)
@@ -1290,17 +1129,18 @@
 
         loop(D // 256, body)
 
+    l_x.wait()
     put_cols(0, colsum(r.dqkv[0]))
     put_cols(1, colsum(r.dqkv[2]))
     if g.wide:
         launch(t_g)
     for n in range(3):
-        grad_rows(r.ds.at[n], r.sb, r.dqkv.at[n])
+        grad_rows(r.ds.at[n], r.x, r.dqkv.at[n])
         launch(t_s[n])
         point()
     cm.rs_start(2, buf, Tl, part5)
     cm.ag_relay(*finals[1][:2])
-    complete(t_c)
+    complete([t_c[n] for n in (3, 1, 2, 0)])
     gather(5, lambda s: r.gc.at[s], save_n(r.gc, r.o_cq, r.o_co))
     r.ge[...] = cm.rs_finish(3, ebuf).astype(BF)
     save(r.ge, r.o_ge)
@@ -1338,21 +1178,37 @@
         cm.ag_drain(10, v_gg)
     for t in tasks:
         cm.g_drain(t)
+    state.drain()
     for d in outs + outs2:
         d.wait()
 
 
-def backward_call(g, lens, out_grad, f):
+def whole_kernel(g, names, *refs):
+    r = types.SimpleNamespace(**dict(zip(names, refs)))
+    state = types.SimpleNamespace(outs=[])
+    forward_body(g, r, Comm(g, r), state)
+    backward_body(g, r, Comm(g, r, 6, 2 + g.D // 256), state)
+
+
+def whole_call(g, ins):
+    names, in_specs, args = [], [], []
+    for n, a in ins.items():
+        names.append(n)
+        args.append(a)
+        if n == LENS:
+            in_specs.append(pl.BlockSpec(memory_space=pltpu.SMEM))
+        elif a.size <= 8 * FJ_MAX:
+            in_specs.append(pl.BlockSpec(memory_space=pltpu.VMEM))
+        else:
+            in_specs.append(ANY)
     D, L, E, Tl, El, S = g.D, g.L, g.E, g.Tl, g.El, g.S
     Dl, DH, FJ, FB = g.Dl, g.DH, g.FJ, g.FB
-    loaded = [n for n in f if n not in PROBS and n != FIRST]
-    names = ["lens", "i_og"] + ["i_" + n for n in f]
-    args = [lens, out_grad] + list(f.values())
-    in_specs = [pl.BlockSpec(memory_space=pltpu.SMEM)] + [ANY] * (len(args) - 1)
     V = pltpu.VMEM
-    scratch = {n: V(f[n].shape, f[n].dtype) for n in loaded}
-    small = (NS, 128) if g.wide else (NS, D)
     outs = dict(
+        lo=((Tl, D), BF),
+        x=((L, D), BF),
+        pbs=((g.H, L, L), BF),
+        pbc=((g.H, L, E), BF),
         gi=((Tl, D), BF),
         ge=((El, D), BF),
         f2=((g.FR, D), BF),
@@ -1361,13 +1217,38 @@
         co=((Dl, D), BF),
         sq=((3, Dl, D), BF),
         so=((Dl, D), BF),
-        small=(small, F32),
+        small=((NS, 128) if g.wide else (NS, D), F32),
     )
     if not g.wide:
         outs.update(fg=((8, FJ), F32))
-        scratch.update(fg=V((8, FJ), F32))
     names += ["o_" + n for n in outs]
-    scratch.update(
+    scratch = dict(
+        lo=V((Tl, D), BF),
+        x=V((L, D), BF),
+        enc=V((E, D), BF),
+        wq=V((3, D, DH), BF),
+        wo=V((DH, D), BF),
+        wc=V((3, D, DH), BF),
+        wd=V((DH, D), BF),
+        w1=V((D, FJ), BF),
+        w2=V((FJ, D), BF),
+        sm=V((NS, D), F32),
+        qkv=V((3, L, DH), BF),
+        sof=V((S, L, DH), BF),
+        fb=V((L, D), BF),
+        cq=V((L, DH), BF),
+        ckv=V((2, E, DH), BF),
+        cof=V((S, L, DH), BF),
+        hid=V((L, FJ), BF),
+        dg=V((L, FJ), BF),
+        h1=V((Tl, D), F32),
+        h2=V((Tl, D), F32),
+        h3=V((Tl, D), F32),
+        rs1=V((Tl, 128), F32),
+        rs2=V((Tl, 128), F32),
+        rs3=V((Tl, 128), F32),
+        bias=V((48, DH), F32),
+        fbv=V((8, FJ), F32),
         gi=V((Tl, D), BF),
         ge=V((El, D), BF),
         g2=V((S, FB, D), BF),
@@ -1400,7 +1281,7 @@
         dqkv=V((3, L, DH), BF),
         dka=V((g.NB, E, 128), F32),
         dva=V((g.NB, E, 128), F32),
-        pbuf=V((2, CH, E), BF),
+        pbuf=V((2 * g.NB, CH, E), BF),
         d2=V((FJ, D), BF),
         d1=V((D, FJ), BF),
         dc=V((4, D, DH), BF),
@@ -1414,8 +1295,12 @@
         zrc=V((4, g.Z - 1, Dl, DH), BF),
         zrs=V((4, g.Z - 1, Dl, DH), BF),
     )
+    if not g.wide:
+        scratch.update(fg=V((8, FJ), F32))
     if g.wide:
         scratch.update(
+            smalls=V((g.R, NS, 128), BF),
+            mine=V((NS, 128), F32),
             yrg=V((g.Y - 1, g.Z, NS, 128), F32),
             zrg=V((g.Z - 1, NS, 128), F32),
             gg=V((S, NS, 128), F32),
@@ -1424,32 +1309,39 @@
     sem = pltpu.SemaphoreType.DMA
     NP = 9 + FJ // 256 + D // 256
     scratch.update(
-        ls=sem((26,)),
+        ls=sem((10,)),
+        lq=sem((g.NB,)),
+        lc=sem((g.NB,)),
+        l1=sem((g.R,)),
+        wzs=sem((NP, g.Z - 1)),
+        wzr=sem((NP, g.Z - 1)),
+        wys=sem((NP, g.Y - 1, g.Z)),
+        wyr=sem((NP, g.Y - 1, g.Z)),
         os=sem((8,)),
-        psem=sem((2,)),
+        psem=sem((2 * g.NB,)),
         fs=sem((7, max(S * (g.R if g.wide else 1), 4 * S * g.NB))),
         gys=sem((NP, g.Y - 1, g.Z)),
         gyr=sem((NP, g.Y - 1, g.Z)),
         gzs=sem((NP, g.Z - 1)),
         gzr=sem((NP, g.Z - 1)),
-        axs=sem((11, g.X - 1)),
-        axr=sem((11, g.X - 1)),
-        acs=sem((11, g.X)),
-        acr=sem((11, g.X)),
-        rcs=sem((4, g.X)),
-        rcr=sem((4, g.X)),
-        rxs=sem((4, g.X - 1)),
-        rxr=sem((4, g.X - 1)),
+        axs=sem((17, g.X - 1)),
+        axr=sem((17, g.X - 1)),
+        acs=sem((17, g.X)),
+        acr=sem((17, g.X)),
+        rcs=sem((6 + D // 256, g.X)),
+        rcr=sem((6 + D // 256, g.X)),
+        rxs=sem((6 + D // 256, g.X - 1)),
+        rxr=sem((6 + D // 256, g.X - 1)),
     )
     names += list(scratch)
     out = pl.pallas_call(
-        functools.partial(backward_kernel, g, names),
+        functools.partial(whole_kernel, g, names),
         out_shape=[jax.ShapeDtypeStruct(*s) for s in outs.values()],
         in_specs=in_specs,
         out_specs=[ANY] * len(outs),
         scratch_shapes=list(scratch.values()),
         compiler_params=pltpu.CompilerParams(
-            collective_id=1, has_side_effects=True, vmem_limit_bytes=67043328
+            collective_id=0, has_side_effects=True, vmem_limit_bytes=67043328
         ),
     )(*args)
     return dict(zip(outs, out))
@@ -1526,6 +1418,7 @@
         lens=lens,
         tok=decoder_in[0],
         states=encoder_states[0],
+        out_grad=out_grad[0],
         self_qkv=self_qkv,
         self_out=self_out,
         cross_qkv=cross_qkv,
@@ -1553,9 +1446,7 @@
             fbias=jnp.broadcast_to(fb.astype(F32), (8, FJ)),
             ffn_in=packed.reshape(Dl, FJ),
         )
-    f = forward_call(g, ins)
-    lo = f.pop(LO)
-    b = types.SimpleNamespace(**backward_call(g, lens, out_grad[0], f))
+    b = types.SimpleNamespace(**whole_call(g, ins))
 
     sm = b.small
     if not g.wide:
@@ -1569,7 +1460,7 @@
     gw1 = b.f1
     if not g.wide:
         gw1 = gw1.reshape(S, Dl, R, FB).transpose(1, 2, 0, 3).reshape(Dl, FF)
-    parts = [(lo, BF), (b.gi, BF), (b.ge, BF)]
+    parts = [(b.lo, BF), (b.gi, BF), (b.ge, BF)]
     parts += [(a, F32) for a in (b.sq, b.so, b.cq, b.co, gw1, b.f2)]
     lo, gi, ge, sq, so, cq, co, f1, f2, gab, gfi, gfo, ggain, gshift = finish_call(g, parts, sm)
     return (

time: 278 us -> 271 us (0.975)
  Pallas kernels: 274 us -> 268 us
    pallas_call x2 -> x1, Pallas kernels: 268 us -> 262 us  [whole_call(): pl.pallas_call(functools.partial(whole_kernel, g, names), out_shape=[jax....]
where the time goes in v2:
time: 271 us
  Pallas kernels  268 us (99%)
    pallas_call x1, Pallas kernels, whole_call(): pl.pallas_call(functools.partial(whole_kernel, g, names), out_shape=[jax....  262 us
    pallas_call x1, Pallas kernels, finish_call(): pl.pallas_call(functools.partial(finish_kernel, cuts), grid=(steps,), out...  6.4 us

profile of v2, /device:TPU:1, one launch (start us, length us, event | category | flops | bytes accessed | tf_op | source)
XLA Modules:
  0.0 271.2 jit_solution(14927285383213821001)
XLA Ops:
  1.9 0.6 pad_add_fusion.refs_0_
  2.5 262.1 %shard_map.263 = (bf16[128,1024]{1,0:T(8,128)(2,1)}, bf16[512,1024]{1,0:T(8,128)(2,1)}, bf16[4,512,512]{2,1,0:T(8,128)(2,1)}, bf16[4,512,1024]{2,1,0:T(8,128)(2,...) custom-call(s32[2]{0:T(128)} %pad_add_fusion.refs_0_, ...), custom_call_target="tpu_custom_call" | custom-call | tf_op jit(solution)/shard_map/pallas_call | solution.py:1337
  264.6 6.4 %shard_map.264 = (bf16[128,1024]{1,0:T(8,128)(2,1)}, bf16[128,1024]{1,0:T(8,128)(2,1)}, bf16[256,1024]{1,0:T(8,128)(2,1)}, f32[3,128,1024]{2,1,0:T(8,128)}, f32[...) custom-call(bf16[128,1024]{1,0:T(8,128)(2,1)} %get-tuple-element.38., ...), custom_call_target="tpu_custom_call" | custom-call | tf_op jit(solution)/shard_map/pallas_call | solution.py:1377

commit v3 on v2

--- a/solution.py
+++ b/solution.py
@@ -23,7 +23,7 @@
 AHEAD = 2
 AHEAD_Y = 2
 PLAN = (1, 1, 1, 1, 2, 1, 1, 1, 1, 1, 1, 0, 1)
-BPLAN = (0, 1, 1, 1, 0, 1, 2, 1, 1, 0, 1, 0, 1, 0, 1, 1, 1, 0, 1, 1)
+BPLAN = (0, 1, 1, 1, 0, 1, 1, 1, 1, 0, 1, 0, 1, 0, 1, 1, 1, 0, 1, 1)
 
 
 def configure(R, S, Tl, El, D, FF):
@@ -976,10 +976,8 @@
         r.dpre[:, cols] = y
         r.fsum[0:1, cols] = colsum(y)
 
-    grad_2(0)
-    launch(t_2[0])
-    loop(n2 - 1, lambda n: grad_2(n + 1))
-    launch(*t_2[1:])
+    loop(2, grad_2)
+    launch(*t_2[:2])
     loop(n1, hidden_back)
     point()
     if g.wide:
@@ -992,6 +990,8 @@
 
     buf = types.SimpleNamespace(part=r.part, acc=r.acc, ps=r.ps, pr=r.pr, xs=r.xs, xr=r.xr)
     cm.rs_start(0, buf, Tl, part3)
+    loop(n2 - 2, lambda n: grad_2(n + 2))
+    launch(*t_2[2:])
     point()
 
     def grad_1(n):

time: 271 us -> 270 us (level)
  no operation moved by 1% of the time
where the time goes in v3:
time: 270 us; the launch traced here: 269 us
  Pallas kernels  267 us (99%)
    pallas_call x1, Pallas kernels, whole_call(): pl.pallas_call(functools.partial(whole_kernel, g, names), out_shape=[jax....  260 us
    pallas_call x1, Pallas kernels, finish_call(): pl.pallas_call(functools.partial(finish_kernel, cuts), grid=(steps,), out...  6.4 us

profile of v3, /device:TPU:1, one launch (start us, length us, event | category | flops | bytes accessed | tf_op | source)
XLA Modules:
  0.0 269.4 jit_solution(1530927936799056994)
XLA Ops:
  1.9 0.6 pad_add_fusion.refs_0_
  2.5 260.3 %shard_map.263 = (bf16[128,1024]{1,0:T(8,128)(2,1)}, bf16[512,1024]{1,0:T(8,128)(2,1)}, bf16[4,512,512]{2,1,0:T(8,128)(2,1)}, bf16[4,512,1024]{2,1,0:T(8,128)(2,...) custom-call(s32[2]{0:T(128)} %pad_add_fusion.refs_0_, ...), custom_call_target="tpu_custom_call" | custom-call | tf_op jit(solution)/shard_map/pallas_call | solution.py:1337
  262.8 6.4 %shard_map.264 = (bf16[128,1024]{1,0:T(8,128)(2,1)}, bf16[128,1024]{1,0:T(8,128)(2,1)}, bf16[256,1024]{1,0:T(8,128)(2,1)}, f32[3,128,1024]{2,1,0:T(8,128)}, f32[...) custom-call(bf16[128,1024]{1,0:T(8,128)(2,1)} %get-tuple-element.38., ...), custom_call_target="tpu_custom_call" | custom-call | tf_op jit(solution)/shard_map/pallas_call | solution.py:1377
